TPU v7x, 128 devices: a whole 4x4x4 slice. The times are simulated.
128 devices in a mesh: row: 8 (over z, x_hi), col: 16 (over y, x_lo, core).
Axes of the slice: x: 4 (x_hi: 2, x_lo: 2; x = x_hi * 2 + x_lo), y: 4, z: 4, core: 2. Of those that a mesh axis runs over, the one named last changes fastest.
Arguments:
- node_feats: bfloat16 [16384, 512], P(('row', 'col')), may hold values from -80 to 80
- block_mask: int32 [128, 128], replicated, may hold values from 0 to 1, as said below
- w_qkv: bfloat16 [2, 512, 1536], replicated, may hold values from -0.25 to 0.25
- w_out: bfloat16 [2, 512, 512], replicated, may hold values from -0.79296875 to 0.79296875
- w_up: bfloat16 [2, 512, 1024], replicated, may hold values from -0.25 to 0.25
- w_down: bfloat16 [2, 1024, 512], replicated, may hold values from -0.1875 to 0.1875
- ln_gain: float32 [2, 2, 512], replicated, may hold values from 0.1 to 1.9
- ln_bias: float32 [2, 2, 512], replicated, may hold values from -3 to 3
Outputs:
- nodes_out: bfloat16 [16384, 512], P(('row', 'col'))
Inputs may be any that keep to these rules, and one draw needn't show every extreme that they name: `block_mask`: A symmetric 0/1 table over the 128 node blocks; every block is linked with itself.
All inputs are finite; a program needn't handle non-finite values.
Results may differ from a plain program's by a relative error of at most 0.022.
Values may be sent and summed in bfloat16 or wider, within the bound.
A program may use at most 128 MiB of HBM per device.

v0:
```python
import jax
import jax.numpy as jnp
from jax import lax
from jax.sharding import PartitionSpec as P

HEADS = 8
BLOCK = 128
LAYERS = 2


def copy_for_each(x, axis):
    length = lax.axis_size(axis)
    return lax.all_to_all(jnp.broadcast_to(x[None], (length, *x.shape)), axis, 0, 0, tiled=True)


def joined_along(tiles, dim):
    lengths = list(tiles.shape[1:])
    lengths[dim] *= tiles.shape[0]
    return jnp.moveaxis(tiles, 0, dim).reshape(lengths)


def gathered_copies(x, axis, dim):
    tiles = copy_for_each(x, axis)
    return joined_along(tiles, dim)


def over_copies(x, axis):
    return copy_for_each(x, axis).max(axis=0)


def split_up(x, dim, length):
    lengths = x.shape
    tiles = x.reshape(*lengths[:dim], length, lengths[dim] // length, *lengths[dim + 1 :])
    return jnp.moveaxis(tiles, dim, 0)


def sent_and_summed(x, axis, dim):
    tiles = split_up(x, dim, lax.axis_size(axis))
    arrived = lax.all_to_all(tiles, axis, split_axis=0, concat_axis=0, tiled=True)
    return arrived.astype(jnp.float32).sum(axis=0)


def side_by_side(arrays, axis, dim, along):
    both = jnp.concatenate(arrays, axis=along)
    whole, at, outs = (sent_and_summed(both, axis, dim), 0, [])
    for a in arrays:
        outs.append(lax.slice_in_dim(whole, at, at + a.shape[along], axis=along))
        at += a.shape[along]
    return tuple(outs)


def layer_norm(values, gain, bias):
    center = values - jnp.mean(values, axis=-1, keepdims=True)
    spread = jnp.mean(center * center, axis=-1, keepdims=True)
    return center * lax.rsqrt(spread + 1e-05) * gain + bias


def per_head(summed, factor):
    count = summed.shape[0]
    return (summed.reshape(count, factor.shape[1], -1) * factor[:, :, None]).reshape(summed.shape)


def partial_attention(queries, keys, values, sub_mask, heads):
    qrows, width = queries.shape
    head_dim = width // heads
    qblock = min(512, qrows)
    nblocks = qrows // qblock
    qsplit = queries.reshape(nblocks, qblock, heads, head_dim)
    ksplit = keys.reshape(-1, heads, head_dim)
    vsplit = values.reshape(-1, heads, head_dim)
    mask_rows = sub_mask.reshape(nblocks, qblock // BLOCK, -1)

    def one_block(item):
        qpart, mpart = item
        scores = jnp.einsum("qhd,khd->hqk", qpart, ksplit, preferred_element_type=jnp.float32) * (
            1.0 / head_dim**0.5
        )
        allowed = (jnp.repeat(jnp.repeat(mpart, BLOCK, axis=0), BLOCK, axis=1) > 0)[None]
        peak = jnp.max(jnp.where(allowed, scores, -1e30), axis=-1, keepdims=True)
        weights = jnp.where(allowed, jnp.exp(scores - peak), 0.0)
        mass = jnp.sum(weights, axis=-1)
        summed = jnp.einsum(
            "hqk,khd->qhd", weights.astype(jnp.bfloat16), vsplit, preferred_element_type=jnp.float32
        )
        return (summed.reshape(qblock, width), peak[:, :, 0].T, mass.T)

    summed, peak, mass = lax.map(one_block, (qsplit, mask_rows))
    return (summed.reshape(qrows, width), peak.reshape(qrows, heads), mass.reshape(qrows, heads))


def per_device(node_feats, block_mask, w_qkv, w_out, w_up, w_down, ln_gain, ln_bias):
    rows, width = node_feats.shape
    heads = HEADS
    n_col = lax.axis_size("col")
    n_row = lax.axis_size("row")
    row_index = lax.axis_index("row")
    col_index = lax.axis_index("col")
    blk_dev = rows // BLOCK
    group_ids = row_index * (n_col * blk_dev) + jnp.arange(n_col * blk_dev, dtype=jnp.int32)
    column_ids = (
        (jnp.arange(n_row, dtype=jnp.int32)[:, None] * n_col + col_index) * blk_dev
        + jnp.arange(blk_dev, dtype=jnp.int32)[None, :]
    ).reshape(-1)
    query_ids, key_ids, own_start = (column_ids, group_ids, row_index * rows)
    sub_mask = jnp.take(jnp.take(block_mask, query_ids, axis=0), key_ids, axis=1)
    x = node_feats
    for layer in range(LAYERS):
        weights = w_qkv[layer]
        own_q = jnp.dot(x, weights[:, :width], preferred_element_type=jnp.float32).astype(
            jnp.bfloat16
        )
        gathered = lax.all_gather(x, "col", axis=0, tiled=True)
        kv_both = jnp.dot(gathered, weights[:, width:], preferred_element_type=jnp.float32).astype(
            jnp.bfloat16
        )
        keys = kv_both[:, :width]
        values = kv_both[:, width:]
        queries = gathered_copies(own_q, "row", 0)
        summed, peak, mass = partial_attention(queries, keys, values, sub_mask, heads)
        top = over_copies(peak.astype(jnp.bfloat16), "row").astype(peak.dtype)
        factor = jnp.exp(peak - top)
        summed, mass = side_by_side(
            (per_head(summed, factor).astype(jnp.bfloat16), (mass * factor).astype(jnp.bfloat16)),
            "row",
            0,
            1,
        )
        attn = per_head(summed, 1.0 / mass).astype(jnp.bfloat16)
        mixed = jnp.dot(attn, w_out[layer], preferred_element_type=jnp.float32)
        hidden = layer_norm(
            x.astype(jnp.float32) + mixed, ln_gain[layer, 0], ln_bias[layer, 0]
        ).astype(jnp.bfloat16)
        up = jax.nn.gelu(jnp.dot(hidden, w_up[layer], preferred_element_type=jnp.float32)).astype(
            jnp.bfloat16
        )
        down = jnp.dot(up, w_down[layer], preferred_element_type=jnp.float32)
        x = layer_norm(
            hidden.astype(jnp.float32) + down, ln_gain[layer, 1], ln_bias[layer, 1]
        ).astype(jnp.bfloat16)
    return x


def solution(mesh):
    placed = (P(("row", "col"), None), P(), P(), P(), P(), P(), P(), P())
    return jax.shard_map(
        per_device, mesh=mesh, in_specs=placed, out_specs=P(("row", "col"), None), check_vma=False
    )
```

profile of v0, /device:TPU:0, one launch (start us, length us, event | category | flops | bytes accessed | tf_op | source)
XLA Modules:
  0.0 401.3 jit_solution(2491265612144790777)
XLA Ops:
  6.5 0.7 all-gather.3.cloned.1.call-update
  7.3 3.3 slice_bitcast_fusion
  10.5 1.1 copy-done.6
  12.0 1.1 broadcast_in_dim.129
  13.1 7.9 %all-to-all-start = ((bf16[8,128,512]{1,2,0:T(8,128)(2,1)}), bf16[8,128,512]{1,2,0:T(8,128)(2,1)S(1)}, u32[]{:S(2)}, u32[]{:S(2)}) async-start(bf16[8,128,512]{1,2,0:T(8,128)(2,1)} %broadcast_in_dim.129), calls=%async_computation | async-start | bytes 2097152 | tf_op jit(solution)/shard_map/all_to_all | solution.py:13
  22.5 24.5 %all-to-all-done = bf16[8,128,512]{1,2,0:T(8,128)(2,1)S(1)} async-done(((bf16[8,128,512]{1,2,0:T(8,128)(2,1)}), bf16[8,128,512]{1,2,0:T(8,128)(2,1)S(1)}, u32[]{:S(2)}, u32[]{:S(2)}) %all-to-all-start) | async-done | bytes 1048608 | tf_op jit(solution)/shard_map/all_to_all | solution.py:13
  47.0 0.7 copy.58
  48.1 1.2 copy.59
  49.9 4.0 convolution_convert_fusion.1
  53.8 1.7 fusion.115
  55.6 1.6 broadcast.253.clone2
  57.2 102.6 %while.28 = (s32[]{:T(128)}, f32[2,512,512]{2,1,0:T(8,128)}, f32[2,512,8]{1,2,0:T(8,128)S(1)}, f32[2,512,8]{1,2,0:T(8,128)S(1)}, s32[2,4,16]{2,1,0:T(4,128)S(1)}...) while((s32[]{:T(128)}, f32[2,512,512]{2,1,0:T(8,128)}, ...), condition=%wide.region_3.4_spmd, body=%wide.region_0.3_spmd.sunk | while | flops 2239750144 | bytes 121259008 | solution.py:87
  57.3 3.5 broadcast_in_dim.180
  60.8 0.6 copy.111
  61.4 13.8 %select_reduce_fusion.4 = (f32[8,512]{1,0:T(8,128)S(1)}, f32[8,512,2048]{2,1,0:T(8,128)}) fusion(pred[512,2048]{1,0:T(8,128)(4,1)S(1)} %bitcast.198, bf16[2048,8,64]{0,2,1:T(8,128)(2,1)S(1)} %get-tuple-element.347, bf16[2,512,8,64]{1,3,2,0:T(8,128)(2,1)S(1)} %copy-done.3, s32[]{:T(128)} %get-tuple-element.332), kind=kOutput, calls=%fused_computation.3.clone.1 | convolution fusion | flops 1098903552 | bytes 37240836 | tf_op jit(solution)/shard_map/while/body/eval_jaxpr/qhd,khd->hqk/dot_general | solution.py:75
  75.2 15.2 %fusion.151 = f32[8,512]{1,0:T(8,128)S(1)} fusion(f32[8,512,2048]{2,1,0:T(8,128)} %get-tuple-element.307, f32[8,512]{1,0:T(8,128)S(1)} %get-tuple-element.308, pred[512,2048]{1,0:T(8,128)(4,1)S(1)} %bitcast.199), kind=kLoop, calls=%fused_computation.4.clone.1 | loop fusion | flops 33550336 | bytes 34635776 | tf_op jit(solution)/shard_map/while/body/eval_jaxpr/reduce_sum | solution.py:81
  90.4 15.5 %fusion.150 = f32[8,512,64]{1,2,0:T(8,128)} fusion(bf16[2048,8,64]{0,2,1:T(8,128)(2,1)} %get-tuple-element.348, f32[8,512,2048]{2,1,0:T(8,128)} %get-tuple-element.307, f32[8,512]{1,0:T(8,128)S(1)} %get-tuple-element.308, pred[512,2048]{1,0:T(8,128)(4,1)S(1)} %bitcast.200), kind=kOutput, calls=%fused_computation.6.clone.1 | convolution fusion | flops 1107296256 | bytes 37765120 | tf_op jit(solution)/shard_map/while/body/eval_jaxpr/hqk,khd->qhd/dot_general | solution.py:82
  105.9 1.6 copy.112
  107.5 1.1 constant_dynamic-update-slice_fusion.4
  108.6 3.5 broadcast_in_dim.180
  112.1 0.6 copy.111
  112.7 13.8 %select_reduce_fusion.4 = (f32[8,512]{1,0:T(8,128)S(1)}, f32[8,512,2048]{2,1,0:T(8,128)}) fusion(pred[512,2048]{1,0:T(8,128)(4,1)S(1)} %bitcast.198, bf16[2048,8,64]{0,2,1:T(8,128)(2,1)S(1)} %get-tuple-element.347, bf16[2,512,8,64]{1,3,2,0:T(8,128)(2,1)S(1)} %copy-done.3, s32[]{:T(128)} %get-tuple-element.332), kind=kOutput, calls=%fused_computation.3.clone.1 | convolution fusion | flops 1098903552 | bytes 37240836 | tf_op jit(solution)/shard_map/while/body/eval_jaxpr/qhd,khd->hqk/dot_general | solution.py:75
  126.5 15.2 %fusion.151 = f32[8,512]{1,0:T(8,128)S(1)} fusion(f32[8,512,2048]{2,1,0:T(8,128)} %get-tuple-element.307, f32[8,512]{1,0:T(8,128)S(1)} %get-tuple-element.308, pred[512,2048]{1,0:T(8,128)(4,1)S(1)} %bitcast.199), kind=kLoop, calls=%fused_computation.4.clone.1 | loop fusion | flops 33550336 | bytes 34635776 | tf_op jit(solution)/shard_map/while/body/eval_jaxpr/reduce_sum | solution.py:81
  141.7 15.5 %fusion.150 = f32[8,512,64]{1,2,0:T(8,128)} fusion(bf16[2048,8,64]{0,2,1:T(8,128)(2,1)} %get-tuple-element.348, f32[8,512,2048]{2,1,0:T(8,128)} %get-tuple-element.307, f32[8,512]{1,0:T(8,128)S(1)} %get-tuple-element.308, pred[512,2048]{1,0:T(8,128)(4,1)S(1)} %bitcast.200), kind=kOutput, calls=%fused_computation.6.clone.1 | convolution fusion | flops 1107296256 | bytes 37765120 | tf_op jit(solution)/shard_map/while/body/eval_jaxpr/hqk,khd->qhd/dot_general | solution.py:82
  157.2 1.6 copy.112
  158.8 1.1 constant_dynamic-update-slice_fusion.4
  159.9 11.7 %all_to_all.30 = bf16[8,1024,8]{1,2,0:T(8,128)(2,1)S(1)} all-to-all(bf16[8,1024,8]{1,2,0:T(8,128)(2,1)S(1)} %broadcast_in_dim.130), channel_id=1, replica_groups=mesh['row'=8,'col'=16] {'row'}, dimensions={0} | all-to-all | bytes 262144 | tf_op jit(solution)/shard_map/all_to_all | solution.py:13
  171.9 1.8 copy.101
  173.7 3.1 copy.61
  177.0 1.9 multiply_convert_fusion.1
  179.1 1.4 copy.63
  180.6 3.6 all-to-all-start.2
  185.6 15.0 %all-to-all-done.2 = bf16[8,128,520]{1,2,0:T(8,128)(2,1)S(1)} async-done(((bf16[8,128,520]{1,2,0:T(8,128)(2,1)}), bf16[8,128,520]{1,2,0:T(8,128)(2,1)S(1)}, u32[]{:S(2)}, u32[]{:S(2)}) %all-to-all-start.2) | async-done | bytes 1064992 | tf_op jit(solution)/shard_map/all_to_all | solution.py:39
  201.7 2.2 fusion.119
  204.1 0.8 add_convert_fusion.2
  205.0 1.4 convolution_convert_fusion.2
  206.6 27.0 %all_to_all.31 = bf16[8,128,512]{1,2,0:T(8,128)(2,1)S(1)} all-to-all(bf16[8,128,512]{1,2,0:T(8,128)(2,1)S(1)} %broadcast_in_dim.131), channel_id=1, replica_groups=mesh['row'=8,'col'=16] {'row'}, dimensions={0} | all-to-all | bytes 2097152 | tf_op jit(solution)/shard_map/all_to_all | solution.py:13
  233.5 0.7 copy.68
  234.7 1.2 copy.69
  235.9 1.0 all-gather.5.cloned.1.call-done
  236.9 4.2 %convolution_convert_fusion = bf16[2048,1024]{0,1:T(8,128)(2,1)S(1)} fusion(bf16[2048,512]{1,0:T(8,128)(2,1)} %all-gather.5.cloned.1.call-done, bf16[512,1536]{1,0:T(8,128)(2,1)} %get-tuple-element.191), kind=kOutput, calls=%fused_computation.38 | convolution fusion | flops 2149580800 | bytes 7340032 | tf_op jit(solution)/shard_map/dot_general | solution.py:113
  241.1 1.7 fusion.114
  242.9 1.6 broadcast.253.clone
  244.5 102.7 %while.29 = (s32[]{:T(128)}, f32[2,512,512]{2,1,0:T(8,128)}, f32[2,512,8]{1,2,0:T(8,128)S(1)}, f32[2,512,8]{1,2,0:T(8,128)S(1)}, s32[2,4,16]{2,1,0:T(4,128)S(1)}...) while((s32[]{:T(128)}, f32[2,512,512]{2,1,0:T(8,128)}, ...), condition=%wide.region_13.14_spmd, body=%wide.region_10.13_spmd.sunk | while | flops 2239750144 | bytes 121259008 | solution.py:87
  244.6 3.5 broadcast_in_dim.188
  248.7 13.8 %select_reduce_fusion.5 = (f32[8,512]{1,0:T(8,128)S(1)}, f32[8,512,2048]{2,1,0:T(8,128)}) fusion(pred[512,2048]{1,0:T(8,128)(4,1)S(1)} %bitcast.201, bf16[2048,8,64]{0,2,1:T(8,128)(2,1)S(1)} %get-tuple-element.374, bf16[2,512,8,64]{1,3,2,0:T(8,128)(2,1)S(1)} %copy-done.2, s32[]{:T(128)} %get-tuple-element.359), kind=kOutput, calls=%fused_computation.21.clone.1 | convolution fusion | flops 1098903552 | bytes 37240836 | tf_op jit(solution)/shard_map/while/body/eval_jaxpr/qhd,khd->hqk/dot_general | solution.py:75
  262.5 15.2 %fusion.157 = f32[8,512]{1,0:T(8,128)S(1)} fusion(f32[8,512,2048]{2,1,0:T(8,128)} %get-tuple-element.319, f32[8,512]{1,0:T(8,128)S(1)} %get-tuple-element.320, pred[512,2048]{1,0:T(8,128)(4,1)S(1)} %bitcast.202), kind=kLoop, calls=%fused_computation.22.clone.1 | loop fusion | flops 33550336 | bytes 34635776 | tf_op jit(solution)/shard_map/while/body/eval_jaxpr/reduce_sum | solution.py:81
  277.7 15.5 %fusion.156 = f32[8,512,64]{1,2,0:T(8,128)} fusion(bf16[2048,8,64]{0,2,1:T(8,128)(2,1)} %get-tuple-element.375, f32[8,512,2048]{2,1,0:T(8,128)} %get-tuple-element.319, f32[8,512]{1,0:T(8,128)S(1)} %get-tuple-element.320, pred[512,2048]{1,0:T(8,128)(4,1)S(1)} %bitcast.203), kind=kOutput, calls=%fused_computation.24.clone.1 | convolution fusion | flops 1107296256 | bytes 37765120 | tf_op jit(solution)/shard_map/while/body/eval_jaxpr/hqk,khd->qhd/dot_general | solution.py:82
  293.2 1.6 copy.114
  294.8 1.1 constant_dynamic-update-slice_fusion.5
  295.9 3.5 broadcast_in_dim.188
  300.0 13.8 %select_reduce_fusion.5 = (f32[8,512]{1,0:T(8,128)S(1)}, f32[8,512,2048]{2,1,0:T(8,128)}) fusion(pred[512,2048]{1,0:T(8,128)(4,1)S(1)} %bitcast.201, bf16[2048,8,64]{0,2,1:T(8,128)(2,1)S(1)} %get-tuple-element.374, bf16[2,512,8,64]{1,3,2,0:T(8,128)(2,1)S(1)} %copy-done.2, s32[]{:T(128)} %get-tuple-element.359), kind=kOutput, calls=%fused_computation.21.clone.1 | convolution fusion | flops 1098903552 | bytes 37240836 | tf_op jit(solution)/shard_map/while/body/eval_jaxpr/qhd,khd->hqk/dot_general | solution.py:75
  313.8 15.2 %fusion.157 = f32[8,512]{1,0:T(8,128)S(1)} fusion(f32[8,512,2048]{2,1,0:T(8,128)} %get-tuple-element.319, f32[8,512]{1,0:T(8,128)S(1)} %get-tuple-element.320, pred[512,2048]{1,0:T(8,128)(4,1)S(1)} %bitcast.202), kind=kLoop, calls=%fused_computation.22.clone.1 | loop fusion | flops 33550336 | bytes 34635776 | tf_op jit(solution)/shard_map/while/body/eval_jaxpr/reduce_sum | solution.py:81
  329.0 15.5 %fusion.156 = f32[8,512,64]{1,2,0:T(8,128)} fusion(bf16[2048,8,64]{0,2,1:T(8,128)(2,1)} %get-tuple-element.375, f32[8,512,2048]{2,1,0:T(8,128)} %get-tuple-element.319, f32[8,512]{1,0:T(8,128)S(1)} %get-tuple-element.320, pred[512,2048]{1,0:T(8,128)(4,1)S(1)} %bitcast.203), kind=kOutput, calls=%fused_computation.24.clone.1 | convolution fusion | flops 1107296256 | bytes 37765120 | tf_op jit(solution)/shard_map/while/body/eval_jaxpr/hqk,khd->qhd/dot_general | solution.py:82
  344.5 1.6 copy.114
  346.1 1.1 constant_dynamic-update-slice_fusion.5
  347.2 14.5 %all_to_all.32 = bf16[8,1024,8]{1,2,0:T(8,128)(2,1)S(1)} all-to-all(bf16[8,1024,8]{1,2,0:T(8,128)(2,1)S(1)} %broadcast_in_dim.132), channel_id=1, replica_groups=mesh['row'=8,'col'=16] {'row'}, dimensions={0} | all-to-all | bytes 262144 | tf_op jit(solution)/shard_map/all_to_all | solution.py:13
  362.0 1.8 copy.102
  363.8 3.1 copy.71
  367.1 1.9 multiply_convert_fusion
  369.2 0.8 copy.73
  370.0 19.3 %all_to_all.33 = bf16[8,128,520]{1,2,0:T(8,128)(2,1)S(1)} all-to-all(bf16[8,128,520]{1,2,0:T(8,128)(2,1)S(1)} %copy.73), channel_id=1, replica_groups=mesh['row'=8,'col'=16] {'row'}, dimensions={0} | all-to-all | bytes 2129920 | tf_op jit(solution)/shard_map/all_to_all | solution.py:39
  391.2 2.2 fusion.123
  393.6 0.8 add_convert_fusion
  (125 shorter events, 10.8 us)
Async XLA Ops:
  6.5 14.5 %copy-start = (s32[128,128]{1,0:T(8,128)S(1)}, s32[128,128]{1,0:T(8,128)}, u32[]{:S(2)}) copy-start(s32[128,128]{1,0:T(8,128)} %param.13) | copy-start | bytes 196612
  6.5 42.7 %all-gather.3.cloned.1.call-start = ((), (), s32[]{:S(2)}) async-start(), calls=%async_computation.6 | async-start | bytes 2228224 | tf_op jit(solution)/shard_map/all_gather | solution.py:112
  7.3 4.4 %copy-start.11 = (bf16[128,512]{1,0:T(8,128)(2,1)S(1)}, bf16[128,512]{1,0:T(8,128)(2,1)}, u32[]{:S(2)}) copy-start(bf16[128,512]{1,0:T(8,128)(2,1)} %param.12) | copy-start | bytes 393220
  10.5 1.1 copy-start.6
  13.1 33.8 %all-to-all-start = ((bf16[8,128,512]{1,2,0:T(8,128)(2,1)}), bf16[8,128,512]{1,2,0:T(8,128)(2,1)S(1)}, u32[]{:S(2)}, u32[]{:S(2)}) async-start(bf16[8,128,512]{1,2,0:T(8,128)(2,1)} %broadcast_in_dim.129), calls=%async_computation | async-start | bytes 2097152 | tf_op jit(solution)/shard_map/all_to_all | solution.py:13
  48.1 1.8 copy-start.7
  57.2 4.2 %copy-start.3 = (bf16[2,512,8,64]{1,3,2,0:T(8,128)(2,1)S(1)}, bf16[2,512,8,64]{1,3,2,0:T(8,128)(2,1)}, u32[]{:S(2)}) copy-start(bf16[2,512,8,64]{1,3,2,0:T(8,128)(2,1)} %get-tuple-element.346) | copy-start | bytes 3145732 | tf_op jit(solution)/shard_map/while
  108.5 4.1 %copy-start.3 = (bf16[2,512,8,64]{1,3,2,0:T(8,128)(2,1)S(1)}, bf16[2,512,8,64]{1,3,2,0:T(8,128)(2,1)}, u32[]{:S(2)}) copy-start(bf16[2,512,8,64]{1,3,2,0:T(8,128)(2,1)} %get-tuple-element.346) | copy-start | bytes 3145732 | tf_op jit(solution)/shard_map/while
  173.7 3.3 copy-start.5
  179.1 5.3 %copy-start.15 = (f32[2,2,512]{2,1,0:T(2,128)S(1)}, f32[2,2,512]{2,1,0:T(2,128)}, u32[]{:S(2)}) copy-start(f32[2,2,512]{2,1,0:T(2,128)} %param.18) | copy-start | bytes 24580
  179.1 5.9 %copy-start.16 = (f32[2,2,512]{2,1,0:T(2,128)S(1)}, f32[2,2,512]{2,1,0:T(2,128)}, u32[]{:S(2)}) copy-start(f32[2,2,512]{2,1,0:T(2,128)} %param.19) | copy-start | bytes 24580
  180.6 20.1 %all-to-all-start.2 = ((bf16[8,128,520]{1,2,0:T(8,128)(2,1)}), bf16[8,128,520]{1,2,0:T(8,128)(2,1)S(1)}, u32[]{:S(2)}, u32[]{:S(2)}) async-start(bf16[8,128,520]{1,2,0:T(8,128)(2,1)} %copy.63), calls=%async_computation.2 | async-start | bytes 2129920 | tf_op jit(solution)/shard_map/all_to_all | solution.py:39
  184.1 17.0 %copy-start.9 = (bf16[2,512,512]{2,1,0:T(8,128)(2,1)S(1)}, bf16[2,512,512]{2,1,0:T(8,128)(2,1)}, u32[]{:S(2)}) copy-start(bf16[2,512,512]{2,1,0:T(8,128)(2,1)} %param.15) | copy-start | bytes 3145732
  184.1 17.0 %copy-start.12 = (bf16[128,512]{1,0:T(8,128)(2,1)S(1)}, bf16[128,512]{1,0:T(8,128)(2,1)}, u32[]{:S(2)}) copy-start(bf16[128,512]{1,0:T(8,128)(2,1)} %param.12) | copy-start | bytes 393220
  184.1 52.8 %all-gather.5.cloned.1.call-start = ((), (), s32[]{:S(2)}) async-start(), calls=%async_computation.7 | async-start | bytes 2228224 | tf_op jit(solution)/shard_map/all_gather | solution.py:112
  244.5 4.2 %copy-start.2 = (bf16[2,512,8,64]{1,3,2,0:T(8,128)(2,1)S(1)}, bf16[2,512,8,64]{1,3,2,0:T(8,128)(2,1)}, u32[]{:S(2)}) copy-start(bf16[2,512,8,64]{1,3,2,0:T(8,128)(2,1)} %get-tuple-element.373) | copy-start | bytes 3145732 | tf_op jit(solution)/shard_map/while
  295.8 4.1 %copy-start.2 = (bf16[2,512,8,64]{1,3,2,0:T(8,128)(2,1)S(1)}, bf16[2,512,8,64]{1,3,2,0:T(8,128)(2,1)}, u32[]{:S(2)}) copy-start(bf16[2,512,8,64]{1,3,2,0:T(8,128)(2,1)} %get-tuple-element.373) | copy-start | bytes 3145732 | tf_op jit(solution)/shard_map/while
  363.8 3.3 copy-start.4
  389.3 0.9 copy-start.8
  389.3 1.3 copy-start.10
  389.4 1.7 copy-start.17
  389.5 1.7 copy-start.18
  391.1 3.3 copy-start.1
  391.2 2.5 copy-start.13
  391.2 2.5 copy-start.14
Sparse Core Ops, SparseCore 0:
  9.0 37.9 all-gather.2
  205.1 31.7 all-gather.4
where the time goes:
time: 403 us; the launch traced here: 401 us
  matrix products  132 us (33%)
  blocking collectives  72.5 us (18%)
  other arithmetic  67.7 us (17%)
  local copies, waits for them, and re-layouts  61.7 us (15%)
  waiting for transfers between devices  41.3 us (10%)
  between operations  13.9 us (3%)
  starting transfers between devices  11.7 us (3%)
    dot_general x4, matrix products, one_block(): jnp.einsum('hqk,khd->qhd', weights.astype(jnp.bfloat16), vsplit, preferre...  62 us
    reduce_sum x4, other arithmetic, one_block(): mass = jnp.sum(weights, axis=-1)  60.7 us
    dot_general x4, matrix products, one_block(): jnp.einsum('qhd,khd->hqk', qpart, ksplit, preferred_element_type=jnp.floa...  55.3 us
    all_to_all x3, blocking collectives, copy_for_each(): lax.all_to_all(jnp.broadcast_to(x[None], (length, *x.shape)), axis, 0, 0,...  53.2 us
    all_to_all x1, waiting for transfers between devices, copy_for_each(): lax.all_to_all(jnp.broadcast_to(x[None], (length, *x.shape)), axis, 0, 0,...  24.5 us
    all_to_all x1, blocking collectives, sent_and_summed(): lax.all_to_all(tiles, axis, split_axis=0, concat_axis=0, tiled=True)  19.3 us
    all_to_all x1, waiting for transfers between devices, sent_and_summed(): lax.all_to_all(tiles, axis, split_axis=0, concat_axis=0, tiled=True)  15 us
    broadcast_in_dim x4, local copies, waits for them, and re-layouts, one_block(): jnp.repeat(jnp.repeat(mpart, BLOCK, axis=0), BLOCK, axis=1) > 0  13.9 us
  transfers between devices with their start and end apart: 4, of which 3 were waited for; matrix products, arithmetic and copies ran while one was open for 3% of the time, Pallas kernels for 0%

commit v1 on v0

v1 whole, which is shorter than its diff:
```python
import functools

import jax
import jax.numpy as jnp
from jax import lax
from jax.experimental import pallas as pl
from jax.experimental.pallas import tpu as pltpu
from jax.sharding import PartitionSpec as P

HEADS = 8
BLOCK = 128
LAYERS = 2
NQ = 8
NK = 16
LOG2E = 1.4426950408889634
LOW = -1e30


def dot_nn(a, b):
    return lax.dot_general(a, b, (((1,), (0,)), ((), ())), preferred_element_type=jnp.float32)


def dot_nt(a, b):
    return lax.dot_general(a, b, (((1,), (1,)), ((), ())), preferred_element_type=jnp.float32)


def layer_norm(values, gain, bias):
    center = values - jnp.mean(values, axis=-1, keepdims=True)
    spread = jnp.mean(center * center, axis=-1, keepdims=True)
    return center * lax.rsqrt(spread + 1e-05) * gain + bias


def attention_kernel(sub_ref, q_ref, k_ref, vt_ref, a_ref, lse_ref, order, qd, acc):
    qd[...] = jnp.zeros_like(qd)

    def one_query_block(r, carry):
        count = jnp.int32(0)
        for k in range(NK):
            order[count] = k
            count = count + sub_ref[r, k]
        for p in range(4):
            qd[p, 0:64, 0:128] = q_ref[r, 128 * p : 128 * p + 64, :]
            qd[p, 64:128, 128:256] = q_ref[r, 128 * p + 64 : 128 * p + 128, :]
        acc[...] = jnp.zeros_like(acc)

        def step(blocks, state):
            out = []
            for p in range(4):
                peak, mass = state[p]
                lanes = slice(128 * p, 128 * p + 128)
                keys = jnp.concatenate([k_ref[b, :, lanes] for b in blocks], axis=0)
                s = dot_nn(keys, qd[p])
                top = jnp.maximum(peak, jnp.max(s, axis=0, keepdims=True))
                fade = jnp.exp2(peak - top)
                w = jnp.exp2(s - top)
                mass = mass * fade + jnp.sum(w, axis=0, keepdims=True)
                values = jnp.concatenate([vt_ref[b, lanes, :] for b in blocks], axis=1)
                o = dot_nn(values, w.astype(jnp.bfloat16))
                lo, hi = slice(128 * p, 128 * p + 64), slice(128 * p + 64, 128 * p + 128)
                acc[lo, :] = acc[lo, :] * fade[:, :128] + o[0:64, 0:128]
                acc[hi, :] = acc[hi, :] * fade[:, 128:] + o[64:128, 128:256]
                out.append((top, mass))
            return tuple(out)

        def pair(i, state):
            return step((order[2 * i], order[2 * i + 1]), state)

        start = tuple(
            (jnp.full((1, 256), LOW, jnp.float32), jnp.zeros((1, 256), jnp.float32))
            for _ in range(4)
        )
        state = lax.fori_loop(0, count // 2, pair, start)
        state = lax.cond(
            count % 2 == 1, lambda s: step((order[jnp.maximum(count - 1, 0)],), s), lambda s: s, state
        )
        for p in range(4):
            peak, mass = state[p]
            some = mass > 0.0
            inv = jnp.where(some, 1.0 / jnp.where(some, mass, 1.0), 0.0)
            lse = jnp.where(some, peak + jnp.log2(jnp.where(some, mass, 1.0)), LOW)
            for h in range(2):
                rows = slice(128 * p + 64 * h, 128 * p + 64 * h + 64)
                side = slice(128 * h, 128 * h + 128)
                a_ref[r, rows, :] = (acc[rows, :] * inv[:, side]).astype(jnp.bfloat16)
                lse_ref[r, 2 * p + h : 2 * p + h + 1, :] = lse[:, side]
        return carry

    lax.fori_loop(0, NQ, one_query_block, 0)


def attention(sub, q, k, vt):
    vmem = pl.BlockSpec(memory_space=pltpu.VMEM)
    return pl.pallas_call(
        attention_kernel,
        out_shape=(
            jax.ShapeDtypeStruct((NQ, 512, 128), jnp.bfloat16),
            jax.ShapeDtypeStruct((NQ, HEADS, 128), jnp.float32),
        ),
        in_specs=[pl.BlockSpec(memory_space=pltpu.SMEM), vmem, vmem, vmem],
        out_specs=(vmem, vmem),
        scratch_shapes=[
            pltpu.SMEM((NK + 1,), jnp.int32),
            pltpu.VMEM((4, 128, 256), jnp.bfloat16),
            pltpu.VMEM((512, 128), jnp.float32),
        ],
    )(sub, q, k, vt)


def per_device(node_feats, block_mask, w_qkv, w_out, w_up, w_down, ln_gain, ln_bias):
    rows, width = node_feats.shape
    row = lax.axis_index("row")
    col = lax.axis_index("col")
    sub = lax.dynamic_index_in_dim(block_mask.reshape(NQ, NK, NQ * NK), col, 1, keepdims=False)
    sub = lax.dynamic_slice_in_dim(sub, row * NK, NK, 1)
    x = node_feats
    for layer in range(LAYERS):
        w = w_qkv[layer]
        qt = (dot_nt(w[:, :width].T, x) * (0.125 * LOG2E)).astype(jnp.bfloat16)
        gathered = lax.all_gather(x, "col", axis=0, tiled=True)
        k = dot_nn(gathered, w[:, width : 2 * width]).astype(jnp.bfloat16).reshape(NK, 128, width)
        vt = jnp.einsum(
            "bni,io->bon", gathered.reshape(NK, 128, width), w[:, 2 * width :],
            preferred_element_type=jnp.float32,
        ).astype(jnp.bfloat16)
        q = lax.all_gather(qt, "row", axis=0, tiled=False)
        a, lse = attention(sub, q, k, vt)
        a = lax.all_to_all(a, "row", 0, 0, tiled=True)
        lse = lax.all_to_all(lse, "row", 0, 0, tiled=True)
        part = jnp.exp2(lse - jnp.max(lse, axis=0, keepdims=True))
        part = part / jnp.sum(part, axis=0, keepdims=True)
        attn = jnp.sum(
            a.reshape(NQ, HEADS, 64, 128).astype(jnp.float32) * part[:, :, None, :], axis=0
        )
        attn = attn.reshape(width, 128).astype(jnp.bfloat16).T
        mixed = jnp.dot(attn, w_out[layer], preferred_element_type=jnp.float32)
        hidden = layer_norm(
            x.astype(jnp.float32) + mixed, ln_gain[layer, 0], ln_bias[layer, 0]
        ).astype(jnp.bfloat16)
        up = jax.nn.gelu(jnp.dot(hidden, w_up[layer], preferred_element_type=jnp.float32)).astype(
            jnp.bfloat16
        )
        down = jnp.dot(up, w_down[layer], preferred_element_type=jnp.float32)
        x = layer_norm(
            hidden.astype(jnp.float32) + down, ln_gain[layer, 1], ln_bias[layer, 1]
        ).astype(jnp.bfloat16)
    return x


def solution(mesh):
    placed = (P(("row", "col"), None), P(), P(), P(), P(), P(), P(), P())
    return jax.shard_map(
        per_device, mesh=mesh, in_specs=placed, out_specs=P(("row", "col"), None), check_vma=False
    )
```

time: 403 us -> 286 us (0.71)
  waiting for transfers between devices: 41.3 us -> 185 us
  matrix products: 132 us -> 21.1 us
  other arithmetic: 67.7 us -> 2.2 us
  local copies, waits for them, and re-layouts: 61.7 us -> 7.17 us
  blocking collectives: 72.5 us -> 26 us
  Pallas kernels: 0 us -> 24 us
  starting transfers between devices: 11.7 us -> 7.24 us
    dot_general x12 -> x6, matrix products: 127 us -> 15.8 us  [the longest x2 8.71 us: per_device(): jnp.einsum('bni,io->bon', gathered.reshape(NK, 128, width), w[:, 2 * widt...]
    all_gather x0 -> x2, waiting for transfers between devices: none -> 87.4 us  [per_device(): q = lax.all_gather(qt, 'row', axis=0, tiled=False)]
    all_gather x2, waiting for transfers between devices: 1.04 us -> 63.4 us  [per_device(): gathered = lax.all_gather(x, 'col', axis=0, tiled=True)]
    reduce_sum x6 -> x4, other arithmetic: 61 us -> 0.45 us  [the longest x2 0.41 us: per_device(): jnp.sum(a.reshape(NQ, HEADS, 64, 128).astype(jnp.float32) * part[:, :, No...]
    all_to_all x4 -> x2, blocking collectives: 72.5 us -> 26 us  [per_device(): lse = lax.all_to_all(lse, 'row', 0, 0, tiled=True)]
    pallas_call x0 -> x2, Pallas kernels: none -> 24 us  [attention(): pl.pallas_call(attention_kernel, out_shape=(jax.ShapeDtypeStruct((NQ, 512...]
    broadcast_in_dim x12 -> x0, local copies, waits for them, and re-layouts: 15.2 us -> none  [the longest x4 13.9 us: one_block(): jnp.repeat(jnp.repeat(mpart, BLOCK, axis=0), BLOCK, axis=1) > 0]
    dynamic_update_slice x12 -> x0, local copies, waits for them, and re-layouts: 10.5 us -> none  [partial_attention(): summed, peak, mass = lax.map(one_block, (qsplit, mask_rows))]
  transfers between devices with their start and end apart: 4 -> 6, of which waited for: 3 -> 6; matrix products, arithmetic and copies ran while one was open for 3% -> 5% of each run, Pallas kernels for 0% -> 0%
where the time goes in v1:
time: 286 us
  waiting for transfers between devices  185 us (65%)
  blocking collectives  26 us (9%)
  Pallas kernels  24 us (8%)
  matrix products  21.1 us (7%)
  between operations  13.4 us (5%)
  starting transfers between devices  7.24 us (3%)
  local copies, waits for them, and re-layouts  7.17 us (3%)
    all_gather x2, waiting for transfers between devices, per_device(): q = lax.all_gather(qt, 'row', axis=0, tiled=False)  87.4 us
    all_gather x2, waiting for transfers between devices, per_device(): gathered = lax.all_gather(x, 'col', axis=0, tiled=True)  63.4 us
    all_to_all x2, waiting for transfers between devices, per_device(): a = lax.all_to_all(a, 'row', 0, 0, tiled=True)  32.6 us
    all_to_all x2, blocking collectives, per_device(): lse = lax.all_to_all(lse, 'row', 0, 0, tiled=True)  26 us
    pallas_call x2, Pallas kernels, attention(): pl.pallas_call(attention_kernel, out_shape=(jax.ShapeDtypeStruct((NQ, 512...  24 us
    dot_general x2, matrix products, per_device(): jnp.einsum('bni,io->bon', gathered.reshape(NK, 128, width), w[:, 2 * widt...  8.71 us
    all_to_all x2, starting transfers between devices, per_device(): a = lax.all_to_all(a, 'row', 0, 0, tiled=True)  7.11 us
  transfers between devices with their start and end apart: 6, of which 6 were waited for; matrix products, arithmetic and copies ran while one was open for 5% of the time, Pallas kernels for 0%

profile of v1, /device:TPU:0, one launch (start us, length us, event | category | flops | bytes accessed | tf_op | source)
XLA Modules:
  0.0 285.8 jit_solution(17632876623851020368)
XLA Ops:
  6.5 0.0 copy-start
  6.5 0.0 all-gather.7.cloned.1.call-start
  6.5 0.7 all-gather.7.cloned.1.call-update
  7.3 0.0 all-gather.11.cloned.1.call-start
  7.3 3.3 %slice_bitcast_fusion = (bf16[512,1536]{1,0:T(8,128)(2,1)}, bf16[1,512,1536]{2,1,0:T(8,128)(2,1)S(1)}) fusion(bf16[2,512,1536]{2,1,0:T(8,128)(2,1)} %param.10), kind=kLoop, calls=%fused_computation.8 | loop fusion | bytes 6291456 | tf_op jit(solution)/shard_map/squeeze | solution.py:117
  10.6 0.0 copy-start.5
  10.6 0.7 copy.16
  11.3 0.2 copy-done.5
  11.5 0.9 fusion.2
  12.4 0.0 all-gather.11.cloned.1.call-update
  12.5 0.0 copy-done
  12.5 0.7 constant_dynamic-slice_fusion
  13.1 32.2 %all-gather.7.cloned.1.call-done = bf16[2048,512]{1,0:T(8,128)(2,1)} async-done(((bf16[128,512]{1,0:T(8,128)(2,1)}), bf16[2048,512]{1,0:T(8,128)(2,1)}) %all-gather.7.cloned.1.call-update) | async-done | bytes 2097168 | tf_op jit(solution)/shard_map/all_gather | solution.py:119
  45.3 0.0 copy-start.8
  45.4 4.3 %convert_bitcast_fusion.1.vt_ref = bf16[16,512,128]{2,1,0:T(8,128)(2,1)} fusion(bf16[16,128,512]{2,1,0:T(8,128)(2,1)} %bitcast.107, bf16[512,1536]{0,1:T(8,128)(2,1)S(1)} %bitcast.94), kind=kOutput, calls=%fused_computation.7 | convolution fusion | flops 1074790400 | bytes 4718592 | tf_op jit(solution)/shard_map/bni,io->bon/dot_general | solution.py:121
  49.7 0.0 copy-done.8
  49.7 2.7 convolution_convert_fusion.1
  52.4 41.8 %all-gather.11.cloned.1.call-done = bf16[4096,128]{1,0:T(8,128)(2,1)} async-done(((bf16[512,128]{1,0:T(8,128)(2,1)}), bf16[4096,128]{1,0:T(8,128)(2,1)}) %all-gather.11.cloned.1.call-update) | async-done | bytes 1048592 | tf_op jit(solution)/shard_map/all_gather | solution.py:125
  94.1 12.0 %shard_map.82 = (bf16[8,512,128]{2,1,0:T(8,128)(2,1)}, f32[8,8,128]{2,1,0:T(8,128)}) custom-call(s32[8,16]{1,0:T(8,128)} %bitcast.97, bf16[8,512,128]{2,1,0:T(8,128)(2,1)} %bitcast.96, bf16[16,128,512]{2,1,0:T(8,128)(2,1)} %bitcast.91, bf16[16,512,128]{2,1,0:T(8,128)(2,1)} %convert_bitcast_fusion.1.vt_ref), custom_call_target="tpu_custom_call" | custom-call | tf_op jit(solution)/shard_map/pallas_call | solution.py:93
  106.1 0.0 copy-start.6
  106.1 0.0 copy-start.7
  106.1 0.0 copy-start.4
  106.1 12.5 %all_to_all.20 = f32[8,8,128]{2,1,0:T(8,128)S(1)} all-to-all(f32[8,8,128]{2,1,0:T(8,128)} %get-tuple-element.10), channel_id=1, replica_groups=mesh['row'=8,'col'=16] {'row'}, dimensions={0} | all-to-all | bytes 65536 | tf_op jit(solution)/shard_map/all_to_all | solution.py:128
  118.5 3.6 %all-to-all-start = ((bf16[8,512,128]{2,1,0:T(8,128)(2,1)}), bf16[8,512,128]{2,1,0:T(8,128)(2,1)S(1)}, u32[]{:S(2)}, u32[]{:S(2)}) async-start(bf16[8,512,128]{2,1,0:T(8,128)(2,1)} %get-tuple-element.9), calls=%async_computation | async-start | bytes 2097152 | tf_op jit(solution)/shard_map/all_to_all | solution.py:127
  122.1 0.0 all-gather.13.cloned.1.call-start
  122.2 0.0 copy-done.6
  122.2 0.0 copy-done.7
  122.3 14.2 %all-to-all-done = bf16[8,512,128]{2,1,0:T(8,128)(2,1)S(1)} async-done(((bf16[8,512,128]{2,1,0:T(8,128)(2,1)}), bf16[8,512,128]{2,1,0:T(8,128)(2,1)S(1)}, u32[]{:S(2)}, u32[]{:S(2)}) %all-to-all-start) | async-done | bytes 1048608 | tf_op jit(solution)/shard_map/all_to_all | solution.py:127
  136.5 0.2 fusion.1
  136.7 0.0 copy-done.4
  136.7 0.3 fusion.91
  137.1 0.2 multiply_reduce_fusion.3
  137.3 0.0 copy-start.1
  137.3 2.4 fusion.92
  139.6 0.2 multiply_reduce_fusion.2
  139.8 0.1 add_convert_fusion.2
  140.0 0.0 copy-start.2
  140.0 0.0 copy-done.1
  140.0 0.9 fusion.4
  140.9 0.0 all-gather.13.cloned.1.call-update
  140.9 0.0 all-gather.9.cloned.1.call-start
  141.0 0.0 copy-done.2
  141.0 0.5 all-gather.9.cloned.1.call-update
  141.5 45.7 %all-gather.13.cloned.1.call-done = bf16[4096,128]{0,1:T(8,128)(2,1)} async-done(((bf16[512,128]{0,1:T(8,128)(2,1)}), bf16[4096,128]{0,1:T(8,128)(2,1)}) %all-gather.13.cloned.1.call-update) | async-done | bytes 1048592 | tf_op jit(solution)/shard_map/all_gather | solution.py:125
  187.2 2.3 copy.13
  189.5 31.2 %all-gather.9.cloned.1.call-done = bf16[2048,512]{1,0:T(8,128)(2,1)} async-done(((bf16[128,512]{1,0:T(8,128)(2,1)}), bf16[2048,512]{1,0:T(8,128)(2,1)}) %all-gather.9.cloned.1.call-update) | async-done | bytes 2097168 | tf_op jit(solution)/shard_map/all_gather | solution.py:119
  220.7 0.0 copy-start.9
  220.7 4.4 %convert_bitcast_fusion.vt_ref = bf16[16,512,128]{2,1,0:T(8,128)(2,1)} fusion(bf16[16,128,512]{2,1,0:T(8,128)(2,1)} %bitcast.108, bf16[512,1536]{1,0:T(8,128)(2,1)S(1)} %copy-done.1), kind=kOutput, calls=%fused_computation.6 | convolution fusion | flops 1074790400 | bytes 4718592 | tf_op jit(solution)/shard_map/bni,io->bon/dot_general | solution.py:121
  225.0 0.0 copy-done.9
  225.0 2.6 convolution_convert_fusion
  227.6 12.0 %shard_map.83 = (bf16[8,512,128]{2,1,0:T(8,128)(2,1)}, f32[8,8,128]{2,1,0:T(8,128)}) custom-call(s32[8,16]{1,0:T(8,128)} %bitcast.98, bf16[8,512,128]{2,1,0:T(8,128)(2,1)} %bitcast.90, bf16[16,128,512]{2,1,0:T(8,128)(2,1)} %bitcast.92, bf16[16,512,128]{2,1,0:T(8,128)(2,1)} %convert_bitcast_fusion.vt_ref), custom_call_target="tpu_custom_call" | custom-call | tf_op jit(solution)/shard_map/pallas_call | solution.py:93
  239.6 0.0 copy-start.3
  239.6 13.6 %all_to_all.21 = f32[8,8,128]{2,1,0:T(8,128)S(1)} all-to-all(f32[8,8,128]{2,1,0:T(8,128)} %get-tuple-element.12), channel_id=1, replica_groups=mesh['row'=8,'col'=16] {'row'}, dimensions={0} | all-to-all | bytes 65536 | tf_op jit(solution)/shard_map/all_to_all | solution.py:128
  253.2 3.6 %all-to-all-start.2 = ((bf16[8,512,128]{2,1,0:T(8,128)(2,1)}), bf16[8,512,128]{2,1,0:T(8,128)(2,1)S(1)}, u32[]{:S(2)}, u32[]{:S(2)}) async-start(bf16[8,512,128]{2,1,0:T(8,128)(2,1)} %get-tuple-element.11), calls=%async_computation.2 | async-start | bytes 2097152 | tf_op jit(solution)/shard_map/all_to_all | solution.py:127
  256.8 18.4 %all-to-all-done.2 = bf16[8,512,128]{2,1,0:T(8,128)(2,1)S(1)} async-done(((bf16[8,512,128]{2,1,0:T(8,128)(2,1)}), bf16[8,512,128]{2,1,0:T(8,128)(2,1)S(1)}, u32[]{:S(2)}, u32[]{:S(2)}) %all-to-all-start.2) | async-done | bytes 1048608 | tf_op jit(solution)/shard_map/all_to_all | solution.py:127
  275.2 0.2 fusion
  275.4 0.0 copy-done.3
  275.5 0.3 fusion.95
  275.8 0.2 multiply_reduce_fusion.1
  276.0 2.2 fusion.96
  278.3 0.2 multiply_reduce_fusion
  278.5 0.8 add_convert_fusion
  (16 shorter events, 0.2 us)
Async XLA Ops:
  6.5 5.9 %copy-start = (s32[128,128]{1,0:T(8,128)S(1)}, s32[128,128]{1,0:T(8,128)}, u32[]{:S(2)}) copy-start(s32[128,128]{1,0:T(8,128)} %param.9) | copy-start | bytes 196612
  6.5 38.8 %all-gather.7.cloned.1.call-start = ((), (), s32[]{:S(2)}) async-start(), calls=%async_computation.4 | async-start | bytes 2228224 | tf_op jit(solution)/shard_map/all_gather | solution.py:119
  7.3 86.9 %all-gather.11.cloned.1.call-start = ((), (), s32[]{:S(2)}) async-start(), calls=%async_computation.6 | async-start | bytes 1179648 | tf_op jit(solution)/shard_map/all_gather | solution.py:125
  10.6 0.9 copy-start.5
  45.3 4.3 %copy-start.8 = (bf16[2048,512]{1,0:T(8,128)(2,1)S(1)}, bf16[2048,512]{1,0:T(8,128)(2,1)}, u32[]{:S(2)}) copy-start(bf16[2048,512]{1,0:T(8,128)(2,1)} %all-gather.7.cloned.1.call-done) | copy-start | bytes 6291460
  106.1 16.1 %copy-start.6 = (f32[2,2,512]{2,1,0:T(2,128)S(1)}, f32[2,2,512]{2,1,0:T(2,128)}, u32[]{:S(2)}) copy-start(f32[2,2,512]{2,1,0:T(2,128)} %param.14) | copy-start | bytes 24580
  106.1 16.1 %copy-start.7 = (f32[2,2,512]{2,1,0:T(2,128)S(1)}, f32[2,2,512]{2,1,0:T(2,128)}, u32[]{:S(2)}) copy-start(f32[2,2,512]{2,1,0:T(2,128)} %param.15) | copy-start | bytes 24580
  106.1 30.6 %copy-start.4 = (bf16[2,512,512]{2,1,0:T(8,128)(2,1)S(1)}, bf16[2,512,512]{2,1,0:T(8,128)(2,1)}, u32[]{:S(2)}) copy-start(bf16[2,512,512]{2,1,0:T(8,128)(2,1)} %param.11) | copy-start | bytes 3145732
  118.5 17.9 %all-to-all-start = ((bf16[8,512,128]{2,1,0:T(8,128)(2,1)}), bf16[8,512,128]{2,1,0:T(8,128)(2,1)S(1)}, u32[]{:S(2)}, u32[]{:S(2)}) async-start(bf16[8,512,128]{2,1,0:T(8,128)(2,1)} %get-tuple-element.9), calls=%async_computation | async-start | bytes 2097152 | tf_op jit(solution)/shard_map/all_to_all | solution.py:127
  122.1 65.1 %all-gather.13.cloned.1.call-start = ((), (), s32[]{:S(2)}) async-start(), calls=%async_computation.7 | async-start | bytes 1179648 | tf_op jit(solution)/shard_map/all_gather | solution.py:125
  137.3 2.7 copy-start.1
  140.0 1.0 copy-start.2
  140.9 79.7 %all-gather.9.cloned.1.call-start = ((), (), s32[]{:S(2)}) async-start(), calls=%async_computation.5 | async-start | bytes 2228224 | tf_op jit(solution)/shard_map/all_gather | solution.py:119
  220.7 4.4 %copy-start.9 = (bf16[2048,512]{1,0:T(8,128)(2,1)S(1)}, bf16[2048,512]{1,0:T(8,128)(2,1)}, u32[]{:S(2)}) copy-start(bf16[2048,512]{1,0:T(8,128)(2,1)} %all-gather.9.cloned.1.call-done) | copy-start | bytes 6291460
  239.6 35.8 %copy-start.3 = (bf16[128,512]{1,0:T(8,128)(2,1)S(1)}, bf16[128,512]{1,0:T(8,128)(2,1)}, u32[]{:S(2)}) copy-start(bf16[128,512]{1,0:T(8,128)(2,1)} %copy-done.2) | copy-start | bytes 393220
  253.2 22.0 %all-to-all-start.2 = ((bf16[8,512,128]{2,1,0:T(8,128)(2,1)}), bf16[8,512,128]{2,1,0:T(8,128)(2,1)S(1)}, u32[]{:S(2)}, u32[]{:S(2)}) async-start(bf16[8,512,128]{2,1,0:T(8,128)(2,1)} %get-tuple-element.11), calls=%async_computation.2 | async-start | bytes 2097152 | tf_op jit(solution)/shard_map/all_to_all | solution.py:127
Sparse Core Ops, SparseCore 0:
  9.0 36.2 all-gather.6
  47.7 46.3 all-gather.10
  141.0 46.0 all-gather.12
  188.7 31.8 all-gather.8

commit v2 on v1

v2 whole, which is shorter than its diff:
```python
import functools

import jax
import jax.numpy as jnp
from jax import lax
from jax.experimental import pallas as pl
from jax.experimental.pallas import tpu as pltpu
from jax.sharding import PartitionSpec as P

HEADS = 8
BLOCK = 128
LAYERS = 2
NQ = 8
NK = 16
LOG2E = 1.4426950408889634
LOW = -1e30
HALF = 64
PACK = 272
MESH = pl.DeviceIdType.MESH


def dot_nn(a, b):
    return lax.dot_general(a, b, (((1,), (0,)), ((), ())), preferred_element_type=jnp.float32)


def dot_nt(a, b):
    return lax.dot_general(a, b, (((1,), (1,)), ((), ())), preferred_element_type=jnp.float32)


def layer_norm(values, gain, bias):
    center = values - jnp.mean(values, axis=-1, keepdims=True)
    spread = jnp.mean(center * center, axis=-1, keepdims=True)
    return center * lax.rsqrt(spread + 1e-05) * gain + bias


def split_lse(lse):
    high = lse.astype(jnp.bfloat16).astype(jnp.float32)
    rest = lse - high
    mid = rest.astype(jnp.bfloat16).astype(jnp.float32)
    low = rest - mid
    return jnp.concatenate([high, mid, low, jnp.zeros_like(low)], axis=0).astype(jnp.bfloat16)


def joined_lse(ref):
    parts = ref[256:272, :].astype(jnp.float32)
    return parts[0:4] + parts[4:8] + parts[8:12]


def attention_kernel(sub_ref, q_ref, k_ref, vt_ref, a_ref, order, qd, acc):
    qd[...] = jnp.zeros_like(qd)

    def one_query_block(r, carry):
        count = jnp.int32(0)
        for k in range(NK):
            order[count] = k
            count = count + sub_ref[r, k]
        for p in range(4):
            qd[p, 0:64, 0:128] = q_ref[r, 128 * p : 128 * p + 64, :]
            qd[p, 64:128, 128:256] = q_ref[r, 128 * p + 64 : 128 * p + 128, :]
        acc[...] = jnp.zeros_like(acc)

        def step(blocks, state):
            out = []
            for p in range(4):
                peak, mass = state[p]
                lanes = slice(128 * p, 128 * p + 128)
                keys = jnp.concatenate([k_ref[b, :, lanes] for b in blocks], axis=0)
                s = dot_nn(keys, qd[p])
                top = jnp.maximum(peak, jnp.max(s, axis=0, keepdims=True))
                fade = jnp.exp2(peak - top)
                w = jnp.exp2(s - top)
                mass = mass * fade + jnp.sum(w, axis=0, keepdims=True)
                values = jnp.concatenate([vt_ref[b, lanes, :] for b in blocks], axis=1)
                o = dot_nn(values, w.astype(jnp.bfloat16))
                lo, hi = slice(128 * p, 128 * p + 64), slice(128 * p + 64, 128 * p + 128)
                acc[lo, :] = acc[lo, :] * fade[:, :128] + o[0:64, 0:128]
                acc[hi, :] = acc[hi, :] * fade[:, 128:] + o[64:128, 128:256]
                out.append((top, mass))
            return tuple(out)

        def pair(i, state):
            return step((order[2 * i], order[2 * i + 1]), state)

        start = tuple(
            (jnp.full((1, 256), LOW, jnp.float32), jnp.zeros((1, 256), jnp.float32))
            for _ in range(4)
        )
        state = lax.fori_loop(0, count // 2, pair, start)
        state = lax.cond(
            count % 2 == 1, lambda s: step((order[jnp.maximum(count - 1, 0)],), s), lambda s: s, state
        )
        for half in range(2):
            found = []
            for p in (2 * half, 2 * half + 1):
                peak, mass = state[p]
                some = mass > 0.0
                safe = jnp.where(some, mass, 1.0)
                inv = jnp.where(some, 1.0 / safe, 0.0)
                lse = jnp.where(some, peak + jnp.log2(safe), LOW)
                for h in range(2):
                    rows = slice(128 * p + 64 * h, 128 * p + 64 * h + 64)
                    here = slice(128 * (p % 2) + 64 * h, 128 * (p % 2) + 64 * h + 64)
                    side = slice(128 * h, 128 * h + 128)
                    a_ref[r, half, here, :] = (acc[rows, :] * inv[:, side]).astype(jnp.bfloat16)
                    found.append(lse[:, side])
            a_ref[r, half, 256:272, :] = split_lse(jnp.concatenate(found, axis=0))
        return carry

    lax.fori_loop(0, NQ, one_query_block, 0)


def attention(sub, q, k, vt):
    vmem = pl.BlockSpec(memory_space=pltpu.VMEM)
    return pl.pallas_call(
        attention_kernel,
        out_shape=jax.ShapeDtypeStruct((NQ, 2, PACK, 128), jnp.bfloat16),
        in_specs=[pl.BlockSpec(memory_space=pltpu.SMEM), vmem, vmem, vmem],
        out_specs=vmem,
        scratch_shapes=[
            pltpu.SMEM((NK + 1,), jnp.int32),
            pltpu.VMEM((4, 128, 256), jnp.bfloat16),
            pltpu.VMEM((512, 128), jnp.float32),
        ],
    )(sub, q, k, vt)


class Place:
    def __init__(self):
        row, col = lax.axis_index("row"), lax.axis_index("col")
        self.z, self.y, self.core = row // 2, col // 4, col % 2
        self.x = (row % 2) * 2 + (col // 2) % 2

    def at(self, x=None, y=None, z=None, core=None):
        x = self.x if x is None else x
        y = self.y if y is None else y % 4
        z = self.z if z is None else z % 4
        core = self.core if core is None else core
        return (z * 2 + x // 2, (y * 2 + x % 2) * 2 + core)


def key_blocks(place):
    out = []
    for c in range(2):
        for dx in range(2):
            for dy in range(4):
                x = place.x if dx == 0 else place.x + 1 - 2 * (place.x % 2)
                core = place.core if c == 0 else 1 - place.core
                row, col = place.at(x=x, y=place.y + dy, core=core)
                out.append(row * 16 + col)
    return out


def query_blocks(place):
    out = []
    for dx in range(2):
        for dz in range(4):
            x = place.x if dx == 0 else 3 - place.x
            row, col = place.at(x=x, z=place.z + dz)
            out.append(row * 16 + col)
    return out


class Wire:
    def __init__(self, send_sem, recv_sem):
        self.send_sem, self.recv_sem, self.copies = send_sem, recv_sem, {}

    def send(self, name, src, dst, to):
        m = len(self.copies)
        copy = pltpu.make_async_remote_copy(
            src_ref=src,
            dst_ref=dst,
            send_sem=self.send_sem.at[m],
            recv_sem=self.recv_sem.at[m],
            device_id=to,
            device_id_type=MESH,
        )
        copy.start()
        self.copies[name] = copy

    def arrived(self, name):
        self.copies[name].wait_recv()

    def drain(self):
        for copy in self.copies.values():
            copy.wait_send()


def merged(refs):
    lses = [joined_lse(ref) for ref in refs]
    top = functools.reduce(jnp.maximum, lses)
    parts = [jnp.exp2(lse - top) for lse in lses]
    total = functools.reduce(jnp.add, parts)
    shares = [part / total for part in parts]
    heads = []
    for h in range(4):
        rows = slice(64 * h, 64 * h + 64)
        heads.append(
            functools.reduce(
                jnp.add,
                [ref[rows, :].astype(jnp.float32) * s[h : h + 1, :] for ref, s in zip(refs, shares)],
            )
        )
    return heads, top + jnp.log2(total)


def merge_into(out, refs):
    heads, lse = merged(refs)
    for h in range(4):
        out[64 * h : 64 * h + 64, :] = heads[h].astype(jnp.bfloat16)
    out[256:272, :] = split_lse(lse)


def reduce_and_mix(wire, peers, a, got, mix, x_ref, weights, gain, bias, spare):
    zp, zm, xq = peers
    w_out, w_up, w_down, ready = weights
    slot = lambda dx, dz, h: a.at[dx * 4 + dz, h]
    for h in range(2):
        wire.send(("x2", h), slot(1, 2, h), got.at[h], xq)
    for h in range(2):
        wire.send(("pm", h), slot(1, 1, h), got.at[2 + h], zp)
        wire.send(("mm", h), slot(1, 3, h), got.at[4 + h], zm)
    wire.arrived(("x2", 0))
    merge_into(mix.at[0], [got.at[0], slot(0, 2, 0)])
    wire.send("cp", mix.at[0], got.at[6], zp)
    wire.arrived(("x2", 1))
    merge_into(mix.at[1], [got.at[1], slot(0, 2, 1)])
    wire.send("cm", mix.at[1], got.at[7], zm)
    wire.send(("zp", 1), slot(0, 1, 1), got.at[8], zp)
    wire.send(("zm", 0), slot(0, 3, 0), got.at[9], zm)
    for h in range(2):
        wire.arrived(("pm", h))
        wire.arrived(("mm", h))
        merge_into(mix.at[2 + h], [got.at[2 + h], got.at[4 + h], slot(1, 0, h)])
        wire.send(("x", h), mix.at[2 + h], got.at[10 + h], xq)
    wire.arrived("cp")
    merge_into(mix.at[4], [got.at[6], slot(0, 1, 0)])
    wire.send(("zp", 0), mix.at[4], got.at[12], zp)
    wire.arrived("cm")
    merge_into(mix.at[5], [got.at[7], slot(0, 3, 1)])
    wire.send(("zm", 1), mix.at[5], got.at[13], zm)
    ends = {0: (12, 9, 10), 1: (8, 13, 11)}
    for h in (1, 0):
        for name in (("zp", h), ("zm", h), ("x", h)):
            wire.arrived(name)
        heads, _ = merged([got.at[i] for i in ends[h]] + [slot(0, 0, h)])
        for i in range(4):
            spare[256 * h + 64 * i : 256 * h + 64 * i + 64, :] = heads[i]
    for i in ready:
        i.wait()
    attn = jnp.concatenate(
        [jnp.transpose(spare[128 * i : 128 * i + 128, :]) for i in range(4)], axis=1
    ).astype(jnp.bfloat16)
    mixed = dot_nn(attn, w_out[...])
    hidden = layer_norm(x_ref[...].astype(jnp.float32) + mixed, gain[0:1], bias[0:1]).astype(jnp.bfloat16)
    up = jax.nn.gelu(dot_nn(hidden, w_up[...])).astype(jnp.bfloat16)
    down = dot_nn(up, w_down[...])
    return layer_norm(hidden.astype(jnp.float32) + down, gain[1:2], bias[1:2]).astype(jnp.bfloat16)


def gather_and_project(wire, peers, x_ref, xg, qg, w, wvt, ready, q_ref, k_ref, vt_ref):
    zp, zm, xq, yp, ym, xk, sib = peers

    def part(ref, h):
        return ref.at[pl.ds(HALF * h, HALF)]

    def key(c, dx, dy, h):
        return xg.at[c * 8 + dx * 4 + dy, pl.ds(HALF * h, HALF)]

    def query(dx, dz, h):
        return qg.at[dx * 4 + dz, pl.ds(256 * h, 256)]

    for h in range(2):
        wire.send(("k", 0, 3, h), part(x_ref, h), key(0, 0, 3, h), yp)
        wire.send(("k", 0, 1, 1 - h), part(x_ref, 1 - h), key(0, 0, 1, 1 - h), ym)
        wire.send(("k", 1, 0, h), part(x_ref, h), key(0, 1, 0, h), xk)
    for h in range(2):
        wire.send(("s", 0, 0, h), part(x_ref, h), key(1, 0, 0, h), sib)
    for i in ready:
        i.wait()
    q = dot_nn(x_ref[...], w[:, 0:512]) * (0.125 * LOG2E)
    for i in range(4):
        qg[0, 128 * i : 128 * i + 128, :] = jnp.transpose(q[:, 128 * i : 128 * i + 128]).astype(
            jnp.bfloat16
        )
    for h in range(2):
        wire.send(("q", 0, 3, h), query(0, 0, h), query(0, 3, h), zp)
        wire.send(("q", 0, 1, 1 - h), query(0, 0, 1 - h), query(0, 1, 1 - h), zm)
        wire.send(("q", 1, 0, h), query(0, 0, h), query(1, 0, h), xq)
    wvt[...] = jnp.transpose(w[:, 1024:1536].astype(jnp.float32)).astype(jnp.bfloat16)

    def project(slots):
        rows = jnp.concatenate(
            [x_ref[...] if s == 0 else xg[s] for s in slots], axis=0
        )
        keys = dot_nn(rows, w[:, 512:1024]).astype(jnp.bfloat16)
        values = dot_nt(wvt[...], rows).astype(jnp.bfloat16)
        for i, s in enumerate(slots):
            k_ref[s] = keys[128 * i : 128 * i + 128]
            vt_ref[s] = values[:, 128 * i : 128 * i + 128]

    def across(dx, dy, h):
        wire.send(("s", dx, dy, h), key(0, dx, dy, h), key(1, dx, dy, h), sib)

    wire.arrived(("k", 0, 3, 0))
    wire.send(("k", 0, 2, 0), key(0, 0, 3, 0), key(0, 0, 2, 0), yp)
    across(0, 3, 0)
    wire.arrived(("k", 0, 1, 1))
    wire.send(("k", 0, 2, 1), key(0, 0, 1, 1), key(0, 0, 2, 1), ym)
    across(0, 1, 1)
    wire.arrived(("k", 1, 0, 0))
    wire.send(("k", 1, 3, 0), key(0, 1, 0, 0), key(0, 1, 3, 0), yp)
    wire.send(("k", 1, 1, 0), key(0, 1, 0, 0), key(0, 1, 1, 0), ym)
    across(1, 0, 0)
    wire.arrived(("q", 0, 3, 0))
    wire.send(("q", 0, 2, 0), query(0, 3, 0), query(0, 2, 0), zp)
    wire.arrived(("q", 0, 1, 1))
    wire.send(("q", 0, 2, 1), query(0, 1, 1), query(0, 2, 1), zm)
    wire.arrived(("q", 1, 0, 0))
    wire.send(("q", 1, 3, 0), query(1, 0, 0), query(1, 3, 0), zp)
    wire.send(("q", 1, 1, 0), query(1, 0, 0), query(1, 1, 0), zm)
    wire.arrived(("k", 1, 0, 1))
    wire.send(("k", 1, 3, 1), key(0, 1, 0, 1), key(0, 1, 3, 1), yp)
    wire.send(("k", 1, 1, 1), key(0, 1, 0, 1), key(0, 1, 1, 1), ym)
    across(1, 0, 1)
    wire.arrived(("k", 0, 3, 1))
    across(0, 3, 1)
    wire.arrived(("k", 0, 1, 0))
    across(0, 1, 0)
    for h in range(2):
        wire.arrived(("s", 0, 0, h))
    project((0, 8))
    wire.arrived(("q", 1, 0, 1))
    wire.send(("q", 1, 3, 1), query(1, 0, 1), query(1, 3, 1), zp)
    wire.send(("q", 1, 1, 1), query(1, 0, 1), query(1, 1, 1), zm)
    wire.arrived(("q", 0, 3, 1))
    wire.arrived(("q", 0, 1, 0))
    for h in range(2):
        wire.arrived(("k", 0, 2, h))
        wire.send(("k", 1, 2, h), key(0, 0, 2, h), key(0, 1, 2, h), xk)
        across(0, 2, h)
    project((1, 3))
    for h in range(2):
        wire.arrived(("q", 0, 2, h))
        wire.send(("q", 1, 2, h), query(0, 2, h), query(1, 2, h), xq)
    project((2, 4))
    for h in range(2):
        wire.arrived(("k", 1, 3, h))
        across(1, 3, h)
        wire.arrived(("k", 1, 1, h))
        across(1, 1, h)
    for h in range(2):
        for dy in (1, 3):
            wire.arrived(("s", 0, dy, h))
    project((9, 11))
    project((5, 7))
    for h in range(2):
        wire.arrived(("k", 1, 2, h))
        across(1, 2, h)
    for h in range(2):
        wire.arrived(("s", 0, 2, h))
        wire.arrived(("s", 1, 0, h))
    project((10, 12))
    for h in range(2):
        for dy in (1, 3):
            wire.arrived(("s", 1, dy, h))
    project((13, 15))
    for h in range(2):
        wire.arrived(("s", 1, 2, h))
    project((6, 14))
    for dz in (1, 2, 3):
        for h in range(2):
            wire.arrived(("q", 1, dz, h))
    q_ref[...] = qg[...]


def link_kernel(layer, reduces, gathers, *refs):
    refs = list(refs)
    x_ref = refs.pop(0)
    if reduces:
        a_ref, w_out_h, w_up_h, w_down_h, gain_ref, bias_ref = refs[:6]
        refs = refs[6:]
    if gathers:
        w_h = refs.pop(0)
    if reduces:
        x_out = refs.pop(0)
    if gathers:
        q_ref, k_ref, vt_ref = refs[:3]
        refs = refs[3:]
    send_sem, recv_sem, copy_sem = refs[:3]
    refs = refs[3:]
    place = Place()
    peers = [
        place.at(z=place.z + 1),
        place.at(z=place.z + 3),
        place.at(x=3 - place.x),
    ]
    if gathers:
        peers += [
            place.at(y=place.y + 1),
            place.at(y=place.y + 3),
            place.at(x=place.x + 1 - 2 * (place.x % 2)),
            place.at(core=1 - place.core),
        ]
    copies = []

    def load(src, dst):
        copy = pltpu.make_async_copy(src, dst, copy_sem.at[len(copies)])
        copy.start()
        copies.append(copy)
        return copy

    if reduces:
        got, mix, spare, w_out, w_up, w_down = refs[:6]
        refs = refs[6:]
        mix_ready = [
            load(w_out_h.at[layer], w_out),
            load(w_up_h.at[layer], w_up),
            load(w_down_h.at[layer], w_down),
        ]
    if gathers:
        xg, qg, w, wvt = refs
        w_ready = [load(w_h.at[layer + 1], w)]
    barrier = pltpu.get_barrier_semaphore()
    for peer in peers:
        pl.semaphore_signal(barrier, inc=1, device_id=peer, device_id_type=MESH)
    pl.semaphore_wait(barrier, len(peers))
    wire = Wire(send_sem, recv_sem)
    if reduces:
        x_out[...] = reduce_and_mix(
            wire, peers[:3], a_ref, got, mix, x_ref, (w_out, w_up, w_down, mix_ready),
            gain_ref[layer], bias_ref[layer], spare,
        )
        x_ref = x_out
    if gathers:
        gather_and_project(wire, peers, x_ref, xg, qg, w, wvt, w_ready, q_ref, k_ref, vt_ref)
    wire.drain()


def link(layer, x, reduce_args=None, w_qkv=None):
    reduces, gathers = reduce_args is not None, w_qkv is not None
    vmem = pl.BlockSpec(memory_space=pltpu.VMEM)
    hbm = pl.BlockSpec(memory_space=pl.ANY)
    args, specs, outs = [x], [vmem], []
    scratch = [
        pltpu.SemaphoreType.DMA((14 * reduces + 44 * gathers,)),
        pltpu.SemaphoreType.DMA((14 * reduces + 44 * gathers,)),
        pltpu.SemaphoreType.DMA((4,)),
    ]
    bf16 = jnp.bfloat16
    if reduces:
        args += list(reduce_args)
        specs += [vmem, hbm, hbm, hbm, vmem, vmem]
        outs.append(jax.ShapeDtypeStruct((128, 512), bf16))
        scratch += [
            pltpu.VMEM((14, PACK, 128), bf16),
            pltpu.VMEM((6, PACK, 128), bf16),
            pltpu.VMEM((512, 128), jnp.float32),
            pltpu.VMEM((512, 512), bf16),
            pltpu.VMEM((512, 1024), bf16),
            pltpu.VMEM((1024, 512), bf16),
        ]
    if gathers:
        args.append(w_qkv)
        specs.append(hbm)
        outs += [
            jax.ShapeDtypeStruct((NQ, 512, 128), bf16),
            jax.ShapeDtypeStruct((NK, 128, 512), bf16),
            jax.ShapeDtypeStruct((NK, 512, 128), bf16),
        ]
        scratch += [
            pltpu.VMEM((NK, 128, 512), bf16),
            pltpu.VMEM((NQ, 512, 128), bf16),
            pltpu.VMEM((512, 1536), bf16),
            pltpu.VMEM((512, 512), bf16),
        ]
    return pl.pallas_call(
        functools.partial(link_kernel, layer, reduces, gathers),
        out_shape=tuple(outs),
        in_specs=specs,
        out_specs=tuple(vmem for _ in outs),
        scratch_shapes=scratch,
        compiler_params=pltpu.CompilerParams(collective_id=layer + 1, has_side_effects=True),
    )(*args)


def per_device(node_feats, block_mask, w_qkv, w_out, w_up, w_down, ln_gain, ln_bias):
    place = Place()
    queries = jnp.stack(query_blocks(place))
    keys = jnp.stack(key_blocks(place))
    sub = block_mask[queries[:, None], keys[None, :]]
    x = node_feats
    q, k, vt = link(-1, x, w_qkv=w_qkv)
    for layer in range(LAYERS):
        parts = attention(sub, q, k, vt)
        last = layer == LAYERS - 1
        rest = (parts, w_out, w_up, w_down, ln_gain, ln_bias)
        if last:
            (x,) = link(layer, x, reduce_args=rest)
        else:
            x, q, k, vt = link(layer, x, reduce_args=rest, w_qkv=w_qkv)
    return x


def solution(mesh):
    placed = (P(("row", "col"), None), P(), P(), P(), P(), P(), P(), P())
    return jax.shard_map(
        per_device, mesh=mesh, in_specs=placed, out_specs=P(("row", "col"), None), check_vma=False
    )
```

time: 286 us -> 109 us (0.38)
  waiting for transfers between devices: 185 us -> 0 us
  Pallas kernels: 24 us -> 105 us
  blocking collectives: 26 us -> 0 us
  matrix products: 21.1 us -> 0 us
  between operations: 13.4 us -> 0.05 us
  starting transfers between devices: 7.24 us -> 0 us
  local copies, waits for them, and re-layouts: 7.17 us -> 4.23 us
    all_gather x4 -> x0, waiting for transfers between devices: 151 us -> none  [the longest x2 87.4 us: per_device(): q = lax.all_gather(qt, 'row', axis=0, tiled=False)]
    pallas_call x2 -> x5, Pallas kernels: 24 us -> 105 us  [the longest x3 84.8 us: link(): pl.pallas_call(functools.partial(link_kernel, layer, reduces, gathers), o...]
    all_to_all x2 -> x0, waiting for transfers between devices: 32.6 us -> none  [per_device(): a = lax.all_to_all(a, 'row', 0, 0, tiled=True)]
    all_to_all x2 -> x0, blocking collectives: 26 us -> none  [per_device(): lse = lax.all_to_all(lse, 'row', 0, 0, tiled=True)]
    dot_general x10 -> x0, matrix products: 21.1 us -> none  [the longest x2 8.71 us: per_device(): jnp.einsum('bni,io->bon', gathered.reshape(NK, 128, width), w[:, 2 * widt...]
    all_to_all x2 -> x0, starting transfers between devices: 7.11 us -> none  [per_device(): a = lax.all_to_all(a, 'row', 0, 0, tiled=True)]
    squeeze x1 -> x0, local copies, waits for them, and re-layouts: 3.26 us -> none  [per_device(): w = w_qkv[layer]]
  transfers between devices with their start and end apart: 6 -> 0, of which waited for: 6 -> 0; matrix products, arithmetic and copies ran while one was open for 5% -> 0% of each run, Pallas kernels for 0% -> 0%
where the time goes in v2:
time: 109 us
  Pallas kernels  105 us (96%)
  local copies, waits for them, and re-layouts  4.23 us (4%)
    pallas_call x3, Pallas kernels, link(): pl.pallas_call(functools.partial(link_kernel, layer, reduces, gathers), o...  84.8 us
    pallas_call x2, Pallas kernels, attention(): pl.pallas_call(attention_kernel, out_shape=jax.ShapeDtypeStruct((NQ, 2, P...  19.9 us

profile of v2, /device:TPU:0, one launch (start us, length us, event | category | flops | bytes accessed | tf_op | source)
XLA Modules:
  0.0 109.1 jit_solution(1930404796873613162)
XLA Ops:
  0.0 0.0 copy-start
  0.0 0.1 stack.103
  0.1 0.1 stack.86
  0.2 0.1 broadcast_or_fusion
  0.3 0.1 reshape.255
  0.4 0.5 copy-done
  0.8 1.2 %gather_fusion = s32[128]{0:T(128)S(1)} fusion(s32[128,128]{1,0:T(8,128)S(1)} %copy-done, s32[128]{0:T(128)S(1)} %reshape.255), kind=kCustom, calls=%fused_computation | custom fusion | bytes 2048 | tf_op jit(solution)/shard_map/gather | solution.py:490
  2.1 0.7 reshape.258.sub_ref
  2.8 23.5 %shard_map.82 = (bf16[8,512,128]{2,1,0:T(8,128)(2,1)}, bf16[16,128,512]{2,1,0:T(8,128)(2,1)}, bf16[16,512,128]{2,1,0:T(8,128)(2,1)}) custom-call(bf16[128,512]{1,0:T(8,128)(2,1)} %refs_0_.3, bf16[2,512,1536]{2,1,0:T(8,128)(2,1)} %refs_7_.1), custom_call_target="tpu_custom_call" | custom-call | tf_op jit(solution)/shard_map/pallas_call | solution.py:476
  26.3 10.0 %shard_map.83.refs_1_ = bf16[8,2,272,128]{3,2,1,0:T(8,128)(2,1)} custom-call(s32[8,16]{1,0:T(8,128)} %reshape.258.sub_ref, bf16[8,512,128]{2,1,0:T(8,128)(2,1)} %get-tuple-element.12.q_ref, bf16[16,128,512]{2,1,0:T(8,128)(2,1)} %get-tuple-element.13.k_ref, bf16[16,512,128]{2,1,0:T(8,128)(2,1)} %get-tuple-element.14.vt_ref), custom_call_target="tpu_custom_call" | custom-call | tf_op jit(solution)/shard_map/pallas_call | solution.py:114
  36.2 39.9 %shard_map.84 = (bf16[128,512]{1,0:T(8,128)(2,1)}, bf16[8,512,128]{2,1,0:T(8,128)(2,1)}, bf16[16,128,512]{2,1,0:T(8,128)(2,1)}, bf16[16,512,128]{2,1,0:T(8,128)(2,1)}) custom-call(bf16[128,512]{1,0:T(8,128)(2,1)} %refs_0_.3, bf16[8,2,272,128]{3,2,1,0:T(8,128)(2,1)} %shard_map.83.refs_1_, bf16[2,512,512]{2,1,0:T(8,128)(2,1)} %refs_2_.3, ...), custom_call_target="tpu_custom_call" | custom-call | tf_op jit(solution)/shard_map/pallas_call | solution.py:476
  76.1 10.0 %shard_map.85.refs_1_ = bf16[8,2,272,128]{3,2,1,0:T(8,128)(2,1)} custom-call(s32[8,16]{1,0:T(8,128)} %reshape.258.sub_ref, bf16[8,512,128]{2,1,0:T(8,128)(2,1)} %get-tuple-element.16.q_ref, bf16[16,128,512]{2,1,0:T(8,128)(2,1)} %get-tuple-element.17.k_ref, bf16[16,512,128]{2,1,0:T(8,128)(2,1)} %get-tuple-element.18.vt_ref), custom_call_target="tpu_custom_call" | custom-call | tf_op jit(solution)/shard_map/pallas_call | solution.py:114
  86.1 21.5 %shard_map.86 = bf16[128,512]{1,0:T(8,128)(2,1)} custom-call(bf16[128,512]{1,0:T(8,128)(2,1)} %get-tuple-element.15.refs_0_, bf16[8,2,272,128]{3,2,1,0:T(8,128)(2,1)} %shard_map.85.refs_1_, bf16[2,512,512]{2,1,0:T(8,128)(2,1)} %refs_2_.3, bf16[2,512,1024]{2,1,0:T(8,128)(2,1)} %refs_3_.3, bf16[2,1024,512]{2,1,0:T(8,128)(2,1)} %refs_4_.3, ...), custom_call_target="tpu_custom_call" | custom-call | tf_op jit(solution)/shard_map/pallas_call | solution.py:476
  107.6 1.6 %copy.10 = bf16[128,512]{1,0:T(8,128)(2,1)} copy(bf16[128,512]{1,0:T(8,128)(2,1)} %shard_map.86) | data formatting | bytes 262144
  (2 shorter events, 0.0 us)
Async XLA Ops:
  0.0 0.8 copy-start

commit v3 on v2

--- a/solution.py
+++ b/solution.py
@@ -46,84 +46,113 @@
     return parts[0:4] + parts[4:8] + parts[8:12]
 
 
-def attention_kernel(sub_ref, q_ref, k_ref, vt_ref, a_ref, order, qd, acc):
-    qd[...] = jnp.zeros_like(qd)
-
-    def one_query_block(r, carry):
-        count = jnp.int32(0)
+def attention_kernel(sub_ref, qd, k_ref, vt_ref, a_ref, order, scores_a, scores_b, tops_a, tops_b, peaks, masses, acc):
+    bank = ((scores_a, tops_a), (scores_b, tops_b))
+    count = jnp.int32(0)
+    for r in range(NQ):
         for k in range(NK):
-            order[count] = k
+            order[count] = 32 * r + k
             count = count + sub_ref[r, k]
+        order[count] = order[jnp.maximum(count - 1, 0)] + 16
+        count = count + count % 2
+    units = count // 2
+    last = jnp.maximum(count - 1, 0)
+    tail = order[last]
+    order[count] = tail - tail % 32 + tail % 16 + 16
+    order[count + 1] = order[count]
+    peaks[...] = jnp.full_like(peaks, LOW)
+    masses[...] = jnp.zeros_like(masses)
+    acc[...] = jnp.zeros_like(acc)
+
+    def decode(u):
+        first, second = order[2 * u], order[2 * u + 1]
+        dead = [jnp.where((code // 16) % 2 == 1, LOW, 0.0) for code in (first, second)]
+        return first // 32, first % 16, second % 16, dead
+
+    def score(u, slot):
+        r, k0, k1, dead = decode(u)
+        scores, tops = bank[slot]
         for p in range(4):
-            qd[p, 0:64, 0:128] = q_ref[r, 128 * p : 128 * p + 64, :]
-            qd[p, 64:128, 128:256] = q_ref[r, 128 * p + 64 : 128 * p + 128, :]
-        acc[...] = jnp.zeros_like(acc)
-
-        def step(blocks, state):
-            out = []
-            for p in range(4):
-                peak, mass = state[p]
-                lanes = slice(128 * p, 128 * p + 128)
-                keys = jnp.concatenate([k_ref[b, :, lanes] for b in blocks], axis=0)
-                s = dot_nn(keys, qd[p])
-                top = jnp.maximum(peak, jnp.max(s, axis=0, keepdims=True))
-                fade = jnp.exp2(peak - top)
-                w = jnp.exp2(s - top)
-                mass = mass * fade + jnp.sum(w, axis=0, keepdims=True)
-                values = jnp.concatenate([vt_ref[b, lanes, :] for b in blocks], axis=1)
-                o = dot_nn(values, w.astype(jnp.bfloat16))
-                lo, hi = slice(128 * p, 128 * p + 64), slice(128 * p + 64, 128 * p + 128)
-                acc[lo, :] = acc[lo, :] * fade[:, :128] + o[0:64, 0:128]
-                acc[hi, :] = acc[hi, :] * fade[:, 128:] + o[64:128, 128:256]
-                out.append((top, mass))
-            return tuple(out)
-
-        def pair(i, state):
-            return step((order[2 * i], order[2 * i + 1]), state)
-
-        start = tuple(
-            (jnp.full((1, 256), LOW, jnp.float32), jnp.zeros((1, 256), jnp.float32))
-            for _ in range(4)
-        )
-        state = lax.fori_loop(0, count // 2, pair, start)
-        state = lax.cond(
-            count % 2 == 1, lambda s: step((order[jnp.maximum(count - 1, 0)],), s), lambda s: s, state
-        )
+            lanes = slice(128 * p, 128 * p + 128)
+            keys = jnp.concatenate([k_ref[k0, :, lanes], k_ref[k1, :, lanes]], axis=0)
+            s = dot_nn(keys, qd[r, p])
+            scores[p] = s
+            top = jnp.maximum(
+                jnp.max(s[0:128], axis=0, keepdims=True) + dead[0],
+                jnp.max(s[128:256], axis=0, keepdims=True) + dead[1],
+            )
+            tops[p : p + 1, :] = top
+
+    def absorb(u, slot):
+        r, k0, k1, dead = decode(u)
+        scores, tops = bank[slot]
+        before = peaks[r]
+        top = jnp.maximum(before, tops[...])
+        fade = jnp.exp2(before - top)
+        peaks[r] = top
+        sums = []
+        for p in range(4):
+            lanes = slice(128 * p, 128 * p + 128)
+            here = top[p : p + 1]
+            w0 = jnp.exp2(scores[p, 0:128] - (here - dead[0]))
+            w1 = jnp.exp2(scores[p, 128:256] - (here - dead[1]))
+            sums.append(jnp.sum(w0, axis=0, keepdims=True) + jnp.sum(w1, axis=0, keepdims=True))
+            w = jnp.concatenate([w0.astype(jnp.bfloat16), w1.astype(jnp.bfloat16)], axis=0)
+            values = jnp.concatenate([vt_ref[k0, lanes, :], vt_ref[k1, lanes, :]], axis=1)
+            o = dot_nn(values, w)
+            lo, hi = slice(128 * p, 128 * p + 64), slice(128 * p + 64, 128 * p + 128)
+            acc[r, lo, :] = acc[r, lo, :] * fade[p : p + 1, :128] + o[0:64, 0:128]
+            acc[r, hi, :] = acc[r, hi, :] * fade[p : p + 1, 128:] + o[64:128, 128:256]
+        masses[r] = masses[r] * fade + jnp.concatenate(sums, axis=0)
+
+    score(0, 0)
+
+    def two_units(i, carry):
+        u = 2 * i
+        score(u + 1, 1)
+        absorb(u, 0)
+        score(jnp.minimum(u + 2, units), 0)
+        absorb(u + 1, 1)
+        return carry
+
+    lax.fori_loop(0, (units + 1) // 2, two_units, 0)
+    for r in range(NQ):
+        mass, peak = masses[r], peaks[r]
+        some = mass > 0.0
+        safe = jnp.where(some, mass, 1.0)
+        inv = jnp.where(some, 1.0 / safe, 0.0)
+        lse = jnp.where(some, peak + jnp.log2(safe), LOW)
         for half in range(2):
             found = []
             for p in (2 * half, 2 * half + 1):
-                peak, mass = state[p]
-                some = mass > 0.0
-                safe = jnp.where(some, mass, 1.0)
-                inv = jnp.where(some, 1.0 / safe, 0.0)
-                lse = jnp.where(some, peak + jnp.log2(safe), LOW)
                 for h in range(2):
                     rows = slice(128 * p + 64 * h, 128 * p + 64 * h + 64)
                     here = slice(128 * (p % 2) + 64 * h, 128 * (p % 2) + 64 * h + 64)
                     side = slice(128 * h, 128 * h + 128)
-                    a_ref[r, half, here, :] = (acc[rows, :] * inv[:, side]).astype(jnp.bfloat16)
-                    found.append(lse[:, side])
+                    a_ref[r, half, here, :] = (acc[r, rows, :] * inv[p : p + 1, side]).astype(jnp.bfloat16)
+                    found.append(lse[p : p + 1, side])
             a_ref[r, half, 256:272, :] = split_lse(jnp.concatenate(found, axis=0))
-        return carry
-
-    lax.fori_loop(0, NQ, one_query_block, 0)
 
 
 def attention(sub, q, k, vt):
     vmem = pl.BlockSpec(memory_space=pltpu.VMEM)
     return pl.pallas_call(
         attention_kernel,
-        out_shape=jax.ShapeDtypeStruct((NQ, 2, PACK, 128), jnp.bfloat16),
+        out_shape=pltpu.VMEM((NQ, 2, PACK, 128), jnp.bfloat16),
         in_specs=[pl.BlockSpec(memory_space=pltpu.SMEM), vmem, vmem, vmem],
         out_specs=vmem,
         scratch_shapes=[
-            pltpu.SMEM((NK + 1,), jnp.int32),
-            pltpu.VMEM((4, 128, 256), jnp.bfloat16),
-            pltpu.VMEM((512, 128), jnp.float32),
+            pltpu.SMEM((NQ * NK + 4,), jnp.int32),
+            pltpu.VMEM((4, 256, 256), jnp.float32),
+            pltpu.VMEM((4, 256, 256), jnp.float32),
+            pltpu.VMEM((4, 256), jnp.float32),
+            pltpu.VMEM((4, 256), jnp.float32),
+            pltpu.VMEM((NQ, 4, 256), jnp.float32),
+            pltpu.VMEM((NQ, 4, 256), jnp.float32),
+            pltpu.VMEM((NQ, 512, 128), jnp.float32),
         ],
+        compiler_params=pltpu.CompilerParams(vmem_limit_bytes=16 * 2**20),
     )(sub, q, k, vt)
-
-
 class Place:
     def __init__(self):
         row, col = lax.axis_index("row"), lax.axis_index("col")
@@ -298,6 +327,17 @@
             k_ref[s] = keys[128 * i : 128 * i + 128]
             vt_ref[s] = values[:, 128 * i : 128 * i + 128]
 
+    def spread_query(s):
+        for p in range(4):
+            q_ref[s, p, 0:64, 0:128] = qg[s, 128 * p : 128 * p + 64, :]
+            q_ref[s, p, 64:128, 128:256] = qg[s, 128 * p + 64 : 128 * p + 128, :]
+
+    off = jnp.zeros((64, 128), jnp.bfloat16)
+    for s in range(NQ):
+        for p in range(4):
+            q_ref[s, p, 0:64, 128:256] = off
+            q_ref[s, p, 64:128, 0:128] = off
+
     def across(dx, dy, h):
         wire.send(("s", dx, dy, h), key(0, dx, dy, h), key(1, dx, dy, h), sib)
 
@@ -342,6 +382,8 @@
     for h in range(2):
         wire.arrived(("q", 0, 2, h))
         wire.send(("q", 1, 2, h), query(0, 2, h), query(1, 2, h), xq)
+    for dz in range(4):
+        spread_query(dz)
     project((2, 4))
     for h in range(2):
         wire.arrived(("k", 1, 3, h))
@@ -370,22 +412,29 @@
     for dz in (1, 2, 3):
         for h in range(2):
             wire.arrived(("q", 1, dz, h))
-    q_ref[...] = qg[...]
+    for dz in range(4):
+        spread_query(4 + dz)
 
 
 def link_kernel(layer, reduces, gathers, *refs):
     refs = list(refs)
     x_ref = refs.pop(0)
+    starts = not reduces
     if reduces:
         a_ref, w_out_h, w_up_h, w_down_h, gain_ref, bias_ref = refs[:6]
         refs = refs[6:]
     if gathers:
         w_h = refs.pop(0)
+    if starts:
+        mask_h = refs.pop(0)
     if reduces:
         x_out = refs.pop(0)
     if gathers:
         q_ref, k_ref, vt_ref = refs[:3]
         refs = refs[3:]
+    if starts:
+        sub_ref = refs.pop(0)
+        mask = refs.pop()
     send_sem, recv_sem, copy_sem = refs[:3]
     refs = refs[3:]
     place = Place()
@@ -420,6 +469,8 @@
     if gathers:
         xg, qg, w, wvt = refs
         w_ready = [load(w_h.at[layer + 1], w)]
+    if starts:
+        mask_ready = load(mask_h, mask)
     barrier = pltpu.get_barrier_semaphore()
     for peer in peers:
         pl.semaphore_signal(barrier, inc=1, device_id=peer, device_id_type=MESH)
@@ -433,13 +484,19 @@
         x_ref = x_out
     if gathers:
         gather_and_project(wire, peers, x_ref, xg, qg, w, wvt, w_ready, q_ref, k_ref, vt_ref)
+    if starts:
+        mask_ready.wait()
+        queries, keys = query_blocks(place), key_blocks(place)
+        for i in range(NQ):
+            for j in range(NK):
+                sub_ref[i, j] = mask[queries[i], keys[j]]
     wire.drain()
 
 
-def link(layer, x, reduce_args=None, w_qkv=None):
+def link(layer, x, reduce_args=None, w_qkv=None, block_mask=None):
     reduces, gathers = reduce_args is not None, w_qkv is not None
     vmem = pl.BlockSpec(memory_space=pltpu.VMEM)
-    hbm = pl.BlockSpec(memory_space=pl.ANY)
+    hbm = pl.BlockSpec(memory_space=pltpu.HBM)
     args, specs, outs = [x], [vmem], []
     scratch = [
         pltpu.SemaphoreType.DMA((14 * reduces + 44 * gathers,)),
@@ -463,9 +520,9 @@
         args.append(w_qkv)
         specs.append(hbm)
         outs += [
-            jax.ShapeDtypeStruct((NQ, 512, 128), bf16),
-            jax.ShapeDtypeStruct((NK, 128, 512), bf16),
-            jax.ShapeDtypeStruct((NK, 512, 128), bf16),
+            pltpu.VMEM((NQ, 4, 128, 256), bf16),
+            pltpu.VMEM((NK, 128, 512), bf16),
+            pltpu.VMEM((NK, 512, 128), bf16),
         ]
         scratch += [
             pltpu.VMEM((NK, 128, 512), bf16),
@@ -473,23 +530,28 @@
             pltpu.VMEM((512, 1536), bf16),
             pltpu.VMEM((512, 512), bf16),
         ]
+    out_specs = [vmem for _ in outs]
+    if not reduces:
+        args.append(block_mask)
+        specs.append(hbm)
+        outs.append(jax.ShapeDtypeStruct((NQ, NK), jnp.int32))
+        out_specs.append(pl.BlockSpec(memory_space=pltpu.SMEM))
+        scratch.append(pltpu.SMEM((128, 128), jnp.int32))
     return pl.pallas_call(
         functools.partial(link_kernel, layer, reduces, gathers),
         out_shape=tuple(outs),
         in_specs=specs,
-        out_specs=tuple(vmem for _ in outs),
+        out_specs=tuple(out_specs),
         scratch_shapes=scratch,
-        compiler_params=pltpu.CompilerParams(collective_id=layer + 1, has_side_effects=True),
+        compiler_params=pltpu.CompilerParams(
+            collective_id=layer + 1, has_side_effects=True, vmem_limit_bytes=24 * 2**20
+        ),
     )(*args)
 
 
 def per_device(node_feats, block_mask, w_qkv, w_out, w_up, w_down, ln_gain, ln_bias):
-    place = Place()
-    queries = jnp.stack(query_blocks(place))
-    keys = jnp.stack(key_blocks(place))
-    sub = block_mask[queries[:, None], keys[None, :]]
     x = node_feats
-    q, k, vt = link(-1, x, w_qkv=w_qkv)
+    q, k, vt, sub = link(-1, x, w_qkv=w_qkv, block_mask=block_mask)
     for layer in range(LAYERS):
         parts = attention(sub, q, k, vt)
         last = layer == LAYERS - 1

time: 109 us -> 82 us (0.75)
  Pallas kernels: 105 us -> 78.4 us
    pallas_call x3, Pallas kernels: 84.8 us -> 71.6 us  [link(): pl.pallas_call(functools.partial(link_kernel, layer, reduces, gathers), o...]
    pallas_call x2, Pallas kernels: 19.9 us -> 6.85 us  [attention(): pl.pallas_call(attention_kernel, out_shape=pltpu.VMEM((NQ, 2, PACK, 128),...]
    unnamed x3 -> x17, local copies, waits for them, and re-layouts: 2.05 us -> 4.32 us
    gather x2 -> x0, local copies, waits for them, and re-layouts: 1.92 us -> none  [per_device(): sub = block_mask[queries[:, None], keys[None, :]]]
where the time goes in v3:
time: 82 us; the launch traced here: 82.9 us
  Pallas kernels  78.4 us (96%)
  local copies, waits for them, and re-layouts  4.32 us (5%)
    pallas_call x3, Pallas kernels, link(): pl.pallas_call(functools.partial(link_kernel, layer, reduces, gathers), o...  71.6 us
    pallas_call x2, Pallas kernels, attention(): pl.pallas_call(attention_kernel, out_shape=pltpu.VMEM((NQ, 2, PACK, 128),...  6.85 us
    unnamed x17, local copies, waits for them, and re-layouts  4.32 us

profile of v3, /device:TPU:0, one launch (start us, length us, event | category | flops | bytes accessed | tf_op | source)
XLA Modules:
  0.0 82.9 jit_solution(11902605059800557105)
XLA Ops:
  0.0 0.0 copy-start
  0.0 1.9 %copy-done = bf16[2,512,1536]{2,1,0:T(8,128)(2,1)S(1)} copy-done((bf16[2,512,1536]{2,1,0:T(8,128)(2,1)S(1)}, bf16[2,512,1536]{2,1,0:T(8,128)(2,1)}, u32[]{:S(2)}) %copy-start) | copy-done | bytes 3145752
  1.9 0.0 copy-start.4
  1.9 0.9 %copy-done.4 = bf16[128,512]{1,0:T(8,128)(2,1)S(1)} copy-done((bf16[128,512]{1,0:T(8,128)(2,1)S(1)}, bf16[128,512]{1,0:T(8,128)(2,1)}, u32[]{:S(2)}) %copy-start.4) | copy-done | bytes 131096
  2.8 0.0 copy-start.5
  2.8 0.8 %copy-done.5 = s32[128,128]{1,0:T(8,128)S(1)} copy-done((s32[128,128]{1,0:T(8,128)S(1)}, s32[128,128]{1,0:T(8,128)}, u32[]{:S(2)}) %copy-start.5) | copy-done | bytes 65560
  3.6 21.4 %shard_map.82 = (bf16[8,4,128,256]{3,2,1,0:T(8,128)(2,1)S(1)}, bf16[16,128,512]{2,1,0:T(8,128)(2,1)S(1)}, bf16[16,512,128]{2,1,0:T(8,128)(2,1)S(1)}, s32[8,16]{1,0:T(8,128)S(1)}) custom-call(bf16[128,512]{1,0:T(8,128)(2,1)S(1)} %copy-done.4, bf16[2,512,1536]{2,1,0:T(8,128)(2,1)S(1)} %copy-done, s32[128,128]{1,0:T(8,128)S(1)} %copy-done.5), custom_call_target="tpu_custom_call" | custom-call | tf_op jit(solution)/shard_map/pallas_call | solution.py:540
  25.0 0.0 copy-start.1
  25.0 0.0 copy-start.2
  25.0 0.0 copy-start.3
  25.0 0.0 copy-start.6
  25.1 0.0 copy-start.7
  25.1 3.4 %shard_map.83.refs_1_ = bf16[8,2,272,128]{3,2,1,0:T(8,128)(2,1)S(1)} custom-call(s32[8,16]{1,0:T(8,128)S(1)} %get-tuple-element.13.sub_ref, bf16[8,4,128,256]{3,2,1,0:T(8,128)(2,1)S(1)} %get-tuple-element.14.qd, bf16[16,128,512]{2,1,0:T(8,128)(2,1)S(1)} %get-tuple-element.15.k_ref, bf16[16,512,128]{2,1,0:T(8,128)(2,1)S(1)} %get-tuple-element.16.vt_ref), custom_call_target="tpu_custom_call" | custom-call | tf_op jit(solution)/shard_map/pallas_call | solution.py:139
  28.5 0.0 copy-done.1
  28.5 0.0 copy-done.2
  28.5 0.0 copy-done.3
  28.5 0.0 copy-done.6
  28.6 0.0 copy-done.7
  28.6 33.1 %shard_map.84 = (bf16[128,512]{1,0:T(8,128)(2,1)S(1)}, bf16[8,4,128,256]{3,2,1,0:T(8,128)(2,1)S(1)}, bf16[16,128,512]{2,1,0:T(8,128)(2,1)S(1)}, bf16[16,512,128]{2,1,0:T(8,128)(2,1)S(1)}) custom-call(bf16[128,512]{1,0:T(8,128)(2,1)S(1)} %copy-done.4, bf16[8,2,272,128]{3,2,1,0:T(8,128)(2,1)S(1)} %shard_map.83.refs_1_, bf16[2,512,512]{2,1,0:T(8,128)(2,1)S(1)} %copy-done.3, ...), custom_call_target="tpu_custom_call" | custom-call | tf_op jit(solution)/shard_map/pallas_call | solution.py:540
  61.6 3.4 %shard_map.85.refs_1_ = bf16[8,2,272,128]{3,2,1,0:T(8,128)(2,1)S(1)} custom-call(s32[8,16]{1,0:T(8,128)S(1)} %get-tuple-element.13.sub_ref, bf16[8,4,128,256]{3,2,1,0:T(8,128)(2,1)S(1)} %get-tuple-element.18.qd, bf16[16,128,512]{2,1,0:T(8,128)(2,1)S(1)} %get-tuple-element.19.k_ref, bf16[16,512,128]{2,1,0:T(8,128)(2,1)S(1)} %get-tuple-element.20.vt_ref), custom_call_target="tpu_custom_call" | custom-call | tf_op jit(solution)/shard_map/pallas_call | solution.py:139
  65.1 17.1 %shard_map.86 = bf16[128,512]{1,0:T(8,128)(2,1)S(1)} custom-call(bf16[128,512]{1,0:T(8,128)(2,1)S(1)} %get-tuple-element.17.refs_0_, bf16[8,2,272,128]{3,2,1,0:T(8,128)(2,1)S(1)} %shard_map.85.refs_1_, bf16[2,512,512]{2,1,0:T(8,128)(2,1)S(1)} %copy-done.3, bf16[2,512,1024]{2,1,0:T(8,128)(2,1)S(1)} %copy-done.1, bf16[2,1024,512]{2,1,0:T(8,128)(2,1)S(1)} %copy-done.2, ...), custom_call_target="tpu_custom_call" | custom-call | tf_op jit(solution)/shard_map/pallas_call | solution.py:540
  82.2 0.7 copy.10
Async XLA Ops:
  0.0 1.9 %copy-start = (bf16[2,512,1536]{2,1,0:T(8,128)(2,1)S(1)}, bf16[2,512,1536]{2,1,0:T(8,128)(2,1)}, u32[]{:S(2)}) copy-start(bf16[2,512,1536]{2,1,0:T(8,128)(2,1)} %refs_7_.1) | copy-start | bytes 9437188
  1.9 0.9 %copy-start.4 = (bf16[128,512]{1,0:T(8,128)(2,1)S(1)}, bf16[128,512]{1,0:T(8,128)(2,1)}, u32[]{:S(2)}) copy-start(bf16[128,512]{1,0:T(8,128)(2,1)} %refs_0_.3) | copy-start | bytes 393220
  2.8 0.8 %copy-start.5 = (s32[128,128]{1,0:T(8,128)S(1)}, s32[128,128]{1,0:T(8,128)}, u32[]{:S(2)}) copy-start(s32[128,128]{1,0:T(8,128)} %refs_2_.3) | copy-start | bytes 196612
  25.0 3.5 %copy-start.1 = (bf16[2,512,1024]{2,1,0:T(8,128)(2,1)S(1)}, bf16[2,512,1024]{2,1,0:T(8,128)(2,1)}, u32[]{:S(2)}) copy-start(bf16[2,512,1024]{2,1,0:T(8,128)(2,1)} %refs_3_.3) | copy-start | bytes 6291460
  25.0 3.5 %copy-start.2 = (bf16[2,1024,512]{2,1,0:T(8,128)(2,1)S(1)}, bf16[2,1024,512]{2,1,0:T(8,128)(2,1)}, u32[]{:S(2)}) copy-start(bf16[2,1024,512]{2,1,0:T(8,128)(2,1)} %refs_4_.3) | copy-start | bytes 6291460
  25.0 3.5 %copy-start.3 = (bf16[2,512,512]{2,1,0:T(8,128)(2,1)S(1)}, bf16[2,512,512]{2,1,0:T(8,128)(2,1)}, u32[]{:S(2)}) copy-start(bf16[2,512,512]{2,1,0:T(8,128)(2,1)} %refs_2_.5) | copy-start | bytes 3145732
  25.0 3.5 %copy-start.6 = (f32[2,2,512]{2,1,0:T(2,128)S(1)}, f32[2,2,512]{2,1,0:T(2,128)}, u32[]{:S(2)}) copy-start(f32[2,2,512]{2,1,0:T(2,128)} %refs_5_.3) | copy-start | bytes 24580
  25.1 3.5 %copy-start.7 = (f32[2,2,512]{2,1,0:T(2,128)S(1)}, f32[2,2,512]{2,1,0:T(2,128)}, u32[]{:S(2)}) copy-start(f32[2,2,512]{2,1,0:T(2,128)} %refs_6_.3) | copy-start | bytes 24580

commit v4 on v3

--- a/solution.py
+++ b/solution.py
@@ -14,8 +14,8 @@
 NK = 16
 LOG2E = 1.4426950408889634
 LOW = -1e30
-HALF = 64
-PACK = 272
+PACK = 144
+PLUS, MINUS = (0, 1), (2, 3)
 MESH = pl.DeviceIdType.MESH
 
 
@@ -38,12 +38,13 @@
     rest = lse - high
     mid = rest.astype(jnp.bfloat16).astype(jnp.float32)
     low = rest - mid
-    return jnp.concatenate([high, mid, low, jnp.zeros_like(low)], axis=0).astype(jnp.bfloat16)
+    pad = jnp.zeros((10, 128), jnp.float32)
+    return jnp.concatenate([high, mid, low, pad], axis=0).astype(jnp.bfloat16)
 
 
 def joined_lse(ref):
-    parts = ref[256:272, :].astype(jnp.float32)
-    return parts[0:4] + parts[4:8] + parts[8:12]
+    parts = ref[128:PACK, :].astype(jnp.float32)
+    return parts[0:2] + parts[2:4] + parts[4:6]
 
 
 def attention_kernel(sub_ref, qd, k_ref, vt_ref, a_ref, order, scores_a, scores_b, tops_a, tops_b, peaks, masses, acc):
@@ -122,23 +123,22 @@
         safe = jnp.where(some, mass, 1.0)
         inv = jnp.where(some, 1.0 / safe, 0.0)
         lse = jnp.where(some, peak + jnp.log2(safe), LOW)
-        for half in range(2):
-            found = []
-            for p in (2 * half, 2 * half + 1):
-                for h in range(2):
-                    rows = slice(128 * p + 64 * h, 128 * p + 64 * h + 64)
-                    here = slice(128 * (p % 2) + 64 * h, 128 * (p % 2) + 64 * h + 64)
-                    side = slice(128 * h, 128 * h + 128)
-                    a_ref[r, half, here, :] = (acc[r, rows, :] * inv[p : p + 1, side]).astype(jnp.bfloat16)
-                    found.append(lse[p : p + 1, side])
-            a_ref[r, half, 256:272, :] = split_lse(jnp.concatenate(found, axis=0))
+        for p in range(4):
+            for h in range(2):
+                rows = slice(128 * p + 64 * h, 128 * p + 64 * h + 64)
+                side = slice(128 * h, 128 * h + 128)
+                a_ref[r, p, 64 * h : 64 * h + 64, :] = (
+                    acc[r, rows, :] * inv[p : p + 1, side]
+                ).astype(jnp.bfloat16)
+            pair = jnp.concatenate([lse[p : p + 1, :128], lse[p : p + 1, 128:]], axis=0)
+            a_ref[r, p, 128:PACK, :] = split_lse(pair)
 
 
 def attention(sub, q, k, vt):
     vmem = pl.BlockSpec(memory_space=pltpu.VMEM)
     return pl.pallas_call(
         attention_kernel,
-        out_shape=pltpu.VMEM((NQ, 2, PACK, 128), jnp.bfloat16),
+        out_shape=pltpu.VMEM((NQ, 4, PACK, 128), jnp.bfloat16),
         in_specs=[pl.BlockSpec(memory_space=pltpu.SMEM), vmem, vmem, vmem],
         out_specs=vmem,
         scratch_shapes=[
@@ -221,7 +221,7 @@
     total = functools.reduce(jnp.add, parts)
     shares = [part / total for part in parts]
     heads = []
-    for h in range(4):
+    for h in range(2):
         rows = slice(64 * h, 64 * h + 64)
         heads.append(
             functools.reduce(
@@ -229,58 +229,63 @@
                 [ref[rows, :].astype(jnp.float32) * s[h : h + 1, :] for ref, s in zip(refs, shares)],
             )
         )
-    return heads, top + jnp.log2(total)
+    return jnp.concatenate(heads, axis=0), top + jnp.log2(total)
 
 
 def merge_into(out, refs):
-    heads, lse = merged(refs)
-    for h in range(4):
-        out[64 * h : 64 * h + 64, :] = heads[h].astype(jnp.bfloat16)
-    out[256:272, :] = split_lse(lse)
-
-
-def reduce_and_mix(wire, peers, a, got, mix, x_ref, weights, gain, bias, spare):
+    both, lse = merged(refs)
+    out[0:128, :] = both.astype(jnp.bfloat16)
+    out[128:PACK, :] = split_lse(lse)
+
+
+def reduce_and_mix(wire, peers, a, got, mix, x_ref, weights, gain, bias):
     zp, zm, xq = peers
     w_out, w_up, w_down, ready = weights
-    slot = lambda dx, dz, h: a.at[dx * 4 + dz, h]
+
+    def slot(dx, dz, j, n=1):
+        return a.at[dx * 4 + dz, pl.ds(j, n)] if n > 1 else a.at[dx * 4 + dz, j]
+
+    def run(ref, j, n=1):
+        return ref.at[pl.ds(j, n)] if n > 1 else ref.at[j]
+
+    for j in (0, 2, 1, 3):
+        wire.send(("x2", j), slot(1, 2, j), run(got, j), xq)
     for h in range(2):
-        wire.send(("x2", h), slot(1, 2, h), got.at[h], xq)
-    for h in range(2):
-        wire.send(("pm", h), slot(1, 1, h), got.at[2 + h], zp)
-        wire.send(("mm", h), slot(1, 3, h), got.at[4 + h], zm)
-    wire.arrived(("x2", 0))
-    merge_into(mix.at[0], [got.at[0], slot(0, 2, 0)])
-    wire.send("cp", mix.at[0], got.at[6], zp)
-    wire.arrived(("x2", 1))
-    merge_into(mix.at[1], [got.at[1], slot(0, 2, 1)])
-    wire.send("cm", mix.at[1], got.at[7], zm)
-    wire.send(("zp", 1), slot(0, 1, 1), got.at[8], zp)
-    wire.send(("zm", 0), slot(0, 3, 0), got.at[9], zm)
+        wire.send(("pm", h), slot(1, 1, 2 * h, 2), run(got, 4 + 2 * h, 2), zp)
+        wire.send(("mm", h), slot(1, 3, 2 * h, 2), run(got, 8 + 2 * h, 2), zm)
+    for j in (0, 2, 1, 3):
+        wire.arrived(("x2", j))
+        merge_into(run(mix, j), [run(got, j), slot(0, 2, j)])
+        wire.send(("c", j), run(mix, j), run(got, 12 + j), zp if j in PLUS else zm)
+    wire.send("zp", slot(0, 1, 2, 2), run(got, 18, 2), zp)
+    wire.send("zm", slot(0, 3, 0, 2), run(got, 20, 2), zm)
     for h in range(2):
         wire.arrived(("pm", h))
         wire.arrived(("mm", h))
-        merge_into(mix.at[2 + h], [got.at[2 + h], got.at[4 + h], slot(1, 0, h)])
-        wire.send(("x", h), mix.at[2 + h], got.at[10 + h], xq)
-    wire.arrived("cp")
-    merge_into(mix.at[4], [got.at[6], slot(0, 1, 0)])
-    wire.send(("zp", 0), mix.at[4], got.at[12], zp)
-    wire.arrived("cm")
-    merge_into(mix.at[5], [got.at[7], slot(0, 3, 1)])
-    wire.send(("zm", 1), mix.at[5], got.at[13], zm)
-    ends = {0: (12, 9, 10), 1: (8, 13, 11)}
-    for h in (1, 0):
-        for name in (("zp", h), ("zm", h), ("x", h)):
-            wire.arrived(name)
-        heads, _ = merged([got.at[i] for i in ends[h]] + [slot(0, 0, h)])
-        for i in range(4):
-            spare[256 * h + 64 * i : 256 * h + 64 * i + 64, :] = heads[i]
+        for j in (2 * h, 2 * h + 1):
+            merge_into(run(mix, 4 + j), [run(got, 4 + j), run(got, 8 + j), slot(1, 0, j)])
+        wire.send(("x", h), run(mix, 4 + 2 * h, 2), run(got, 24 + 2 * h, 2), xq)
+    for j in (0, 2, 1, 3):
+        wire.arrived(("c", j))
+        if j in PLUS:
+            merge_into(run(mix, 8 + j), [run(got, 12 + j), slot(0, 1, j)])
+            wire.send(("z", j), run(mix, 8 + j), run(got, 16 + j), zp)
+        else:
+            merge_into(run(mix, 8 + j), [run(got, 12 + j), slot(0, 3, j)])
+            wire.send(("z", j), run(mix, 8 + j), run(got, 20 + j), zm)
     for i in ready:
         i.wait()
-    attn = jnp.concatenate(
-        [jnp.transpose(spare[128 * i : 128 * i + 128, :]) for i in range(4)], axis=1
-    ).astype(jnp.bfloat16)
-    mixed = dot_nn(attn, w_out[...])
-    hidden = layer_norm(x_ref[...].astype(jnp.float32) + mixed, gain[0:1], bias[0:1]).astype(jnp.bfloat16)
+    mixed = x_ref[...].astype(jnp.float32)
+    wire.arrived("zp")
+    wire.arrived("zm")
+    wire.arrived(("x", 0))
+    wire.arrived(("x", 1))
+    for j in (0, 2, 1, 3):
+        wire.arrived(("z", j))
+        both, _ = merged([run(got, 16 + j), run(got, 20 + j), run(got, 24 + j), slot(0, 0, j)])
+        attn = jnp.transpose(both).astype(jnp.bfloat16)
+        mixed = mixed + dot_nn(attn, w_out[128 * j : 128 * j + 128, :])
+    hidden = layer_norm(mixed, gain[0:1], bias[0:1]).astype(jnp.bfloat16)
     up = jax.nn.gelu(dot_nn(hidden, w_up[...])).astype(jnp.bfloat16)
     down = dot_nn(up, w_down[...])
     return layer_norm(hidden.astype(jnp.float32) + down, gain[1:2], bias[1:2]).astype(jnp.bfloat16)
@@ -289,21 +294,25 @@
 def gather_and_project(wire, peers, x_ref, xg, qg, w, wvt, ready, q_ref, k_ref, vt_ref):
     zp, zm, xq, yp, ym, xk, sib = peers
 
-    def part(ref, h):
-        return ref.at[pl.ds(HALF * h, HALF)]
-
-    def key(c, dx, dy, h):
-        return xg.at[c * 8 + dx * 4 + dy, pl.ds(HALF * h, HALF)]
-
-    def query(dx, dz, h):
-        return qg.at[dx * 4 + dz, pl.ds(256 * h, 256)]
-
-    for h in range(2):
-        wire.send(("k", 0, 3, h), part(x_ref, h), key(0, 0, 3, h), yp)
-        wire.send(("k", 0, 1, 1 - h), part(x_ref, 1 - h), key(0, 0, 1, 1 - h), ym)
-        wire.send(("k", 1, 0, h), part(x_ref, h), key(0, 1, 0, h), xk)
-    for h in range(2):
-        wire.send(("s", 0, 0, h), part(x_ref, h), key(1, 0, 0, h), sib)
+    def part(ref, j, n=1):
+        return ref.at[pl.ds(32 * j, 32 * n)]
+
+    def key(c, dx, dy, j=0, n=4):
+        return xg.at[c * 8 + dx * 4 + dy, pl.ds(32 * j, 32 * n)]
+
+    def query(dx, dz, j=0, n=4):
+        return qg.at[dx * 4 + dz, pl.ds(128 * j, 128 * n)]
+
+    def across(dx, dy, j=0, n=4):
+        wire.send(("s", dx, dy, j), key(0, dx, dy, j, n), key(1, dx, dy, j, n), sib)
+
+    for i in range(4):
+        j = (i + 2) % 4
+        wire.send(("k", 0, 3, i), part(x_ref, i), key(0, 0, 3, i, 1), yp)
+        wire.send(("k", 0, 1, j), part(x_ref, j), key(0, 0, 1, j, 1), ym)
+        if i % 2 == 0:
+            wire.send(("k", 1, 0, i), part(x_ref, i, 2), key(0, 1, 0, i, 2), xk)
+    wire.send(("s", 0, 0, 0), part(x_ref, 0, 4), key(1, 0, 0), sib)
     for i in ready:
         i.wait()
     q = dot_nn(x_ref[...], w[:, 0:512]) * (0.125 * LOG2E)
@@ -311,16 +320,21 @@
         qg[0, 128 * i : 128 * i + 128, :] = jnp.transpose(q[:, 128 * i : 128 * i + 128]).astype(
             jnp.bfloat16
         )
-    for h in range(2):
-        wire.send(("q", 0, 3, h), query(0, 0, h), query(0, 3, h), zp)
-        wire.send(("q", 0, 1, 1 - h), query(0, 0, 1 - h), query(0, 1, 1 - h), zm)
-        wire.send(("q", 1, 0, h), query(0, 0, h), query(1, 0, h), xq)
+    for i in range(4):
+        j = (i + 2) % 4
+        wire.send(("q", 0, 3, i), query(0, 0, i, 1), query(0, 3, i, 1), zp)
+        wire.send(("q", 0, 1, j), query(0, 0, j, 1), query(0, 1, j, 1), zm)
+        if i % 2 == 0:
+            wire.send(("q", 1, 0, i), query(0, 0, i, 2), query(1, 0, i, 2), xq)
     wvt[...] = jnp.transpose(w[:, 1024:1536].astype(jnp.float32)).astype(jnp.bfloat16)
+    off = jnp.zeros((64, 128), jnp.bfloat16)
+    for s in range(NQ):
+        for p in range(4):
+            q_ref[s, p, 0:64, 128:256] = off
+            q_ref[s, p, 64:128, 0:128] = off
 
     def project(slots):
-        rows = jnp.concatenate(
-            [x_ref[...] if s == 0 else xg[s] for s in slots], axis=0
-        )
+        rows = jnp.concatenate([x_ref[...] if s == 0 else xg[s] for s in slots], axis=0)
         keys = dot_nn(rows, w[:, 512:1024]).astype(jnp.bfloat16)
         values = dot_nt(wvt[...], rows).astype(jnp.bfloat16)
         for i, s in enumerate(slots):
@@ -332,86 +346,69 @@
             q_ref[s, p, 0:64, 0:128] = qg[s, 128 * p : 128 * p + 64, :]
             q_ref[s, p, 64:128, 128:256] = qg[s, 128 * p + 64 : 128 * p + 128, :]
 
-    off = jnp.zeros((64, 128), jnp.bfloat16)
-    for s in range(NQ):
-        for p in range(4):
-            q_ref[s, p, 0:64, 128:256] = off
-            q_ref[s, p, 64:128, 0:128] = off
-
-    def across(dx, dy, h):
-        wire.send(("s", dx, dy, h), key(0, dx, dy, h), key(1, dx, dy, h), sib)
-
-    wire.arrived(("k", 0, 3, 0))
-    wire.send(("k", 0, 2, 0), key(0, 0, 3, 0), key(0, 0, 2, 0), yp)
-    across(0, 3, 0)
-    wire.arrived(("k", 0, 1, 1))
-    wire.send(("k", 0, 2, 1), key(0, 0, 1, 1), key(0, 0, 2, 1), ym)
-    across(0, 1, 1)
-    wire.arrived(("k", 1, 0, 0))
-    wire.send(("k", 1, 3, 0), key(0, 1, 0, 0), key(0, 1, 3, 0), yp)
-    wire.send(("k", 1, 1, 0), key(0, 1, 0, 0), key(0, 1, 1, 0), ym)
-    across(1, 0, 0)
-    wire.arrived(("q", 0, 3, 0))
-    wire.send(("q", 0, 2, 0), query(0, 3, 0), query(0, 2, 0), zp)
-    wire.arrived(("q", 0, 1, 1))
-    wire.send(("q", 0, 2, 1), query(0, 1, 1), query(0, 2, 1), zm)
-    wire.arrived(("q", 1, 0, 0))
-    wire.send(("q", 1, 3, 0), query(1, 0, 0), query(1, 3, 0), zp)
-    wire.send(("q", 1, 1, 0), query(1, 0, 0), query(1, 1, 0), zm)
-    wire.arrived(("k", 1, 0, 1))
-    wire.send(("k", 1, 3, 1), key(0, 1, 0, 1), key(0, 1, 3, 1), yp)
-    wire.send(("k", 1, 1, 1), key(0, 1, 0, 1), key(0, 1, 1, 1), ym)
-    across(1, 0, 1)
-    wire.arrived(("k", 0, 3, 1))
-    across(0, 3, 1)
-    wire.arrived(("k", 0, 1, 0))
-    across(0, 1, 0)
-    for h in range(2):
-        wire.arrived(("s", 0, 0, h))
+    for i in range(2):
+        wire.arrived(("k", 0, 3, i))
+        wire.send(("k", 0, 2, i), key(0, 0, 3, i, 1), key(0, 0, 2, i, 1), yp)
+        wire.arrived(("k", 0, 1, 2 + i))
+        wire.send(("k", 0, 2, 2 + i), key(0, 0, 1, 2 + i, 1), key(0, 0, 2, 2 + i, 1), ym)
+    for i in range(2):
+        wire.arrived(("q", 0, 3, i))
+        wire.send(("q", 0, 2, i), query(0, 3, i, 1), query(0, 2, i, 1), zp)
+        wire.arrived(("q", 0, 1, 2 + i))
+        wire.send(("q", 0, 2, 2 + i), query(0, 1, 2 + i, 1), query(0, 2, 2 + i, 1), zm)
+    for i in (0, 2):
+        wire.arrived(("k", 1, 0, i))
+        wire.send(("k", 1, 3, i), key(0, 1, 0, i, 2), key(0, 1, 3, i, 2), yp)
+        wire.send(("k", 1, 1, i), key(0, 1, 0, i, 2), key(0, 1, 1, i, 2), ym)
+        wire.arrived(("q", 1, 0, i))
+        wire.send(("q", 1, 3, i), query(1, 0, i, 2), query(1, 3, i, 2), zp)
+        wire.send(("q", 1, 1, i), query(1, 0, i, 2), query(1, 1, i, 2), zm)
+    across(1, 0)
+    for i in range(2):
+        wire.arrived(("k", 0, 3, 2 + i))
+        wire.arrived(("k", 0, 1, i))
+    across(0, 3)
+    across(0, 1)
+    wire.arrived(("s", 0, 0, 0))
     project((0, 8))
-    wire.arrived(("q", 1, 0, 1))
-    wire.send(("q", 1, 3, 1), query(1, 0, 1), query(1, 3, 1), zp)
-    wire.send(("q", 1, 1, 1), query(1, 0, 1), query(1, 1, 1), zm)
-    wire.arrived(("q", 0, 3, 1))
-    wire.arrived(("q", 0, 1, 0))
-    for h in range(2):
-        wire.arrived(("k", 0, 2, h))
-        wire.send(("k", 1, 2, h), key(0, 0, 2, h), key(0, 1, 2, h), xk)
-        across(0, 2, h)
+    for j in (0, 2, 1, 3):
+        wire.arrived(("k", 0, 2, j))
+        wire.send(("k", 1, 2, j), key(0, 0, 2, j, 1), key(0, 1, 2, j, 1), xk)
+    across(0, 2)
+    for j in (0, 2, 1, 3):
+        wire.arrived(("q", 0, 2, j))
+        wire.send(("q", 1, 2, j), query(0, 2, j, 1), query(1, 2, j, 1), xq)
     project((1, 3))
-    for h in range(2):
-        wire.arrived(("q", 0, 2, h))
-        wire.send(("q", 1, 2, h), query(0, 2, h), query(1, 2, h), xq)
+    project((2, 4))
+    for i in range(2):
+        wire.arrived(("q", 0, 3, 2 + i))
+        wire.arrived(("q", 0, 1, i))
     for dz in range(4):
         spread_query(dz)
-    project((2, 4))
-    for h in range(2):
-        wire.arrived(("k", 1, 3, h))
-        across(1, 3, h)
-        wire.arrived(("k", 1, 1, h))
-        across(1, 1, h)
-    for h in range(2):
+    for dx, dy in ((1, 0), (0, 3), (0, 1), (0, 2)):
+        wire.arrived(("s", dx, dy, 0))
+    project((9, 11))
+    for i in (0, 2):
         for dy in (1, 3):
-            wire.arrived(("s", 0, dy, h))
-    project((9, 11))
+            wire.arrived(("k", 1, dy, i))
+            across(1, dy, i, 2)
+    project((10, 12))
+    for j in (0, 2, 1, 3):
+        wire.arrived(("k", 1, 2, j))
+        across(1, 2, j, 1)
     project((5, 7))
-    for h in range(2):
-        wire.arrived(("k", 1, 2, h))
-        across(1, 2, h)
-    for h in range(2):
-        wire.arrived(("s", 0, 2, h))
-        wire.arrived(("s", 1, 0, h))
-    project((10, 12))
-    for h in range(2):
+    for i in (0, 2):
         for dy in (1, 3):
-            wire.arrived(("s", 1, dy, h))
+            wire.arrived(("s", 1, dy, i))
     project((13, 15))
-    for h in range(2):
-        wire.arrived(("s", 1, 2, h))
+    for j in (0, 2, 1, 3):
+        wire.arrived(("s", 1, 2, j))
     project((6, 14))
-    for dz in (1, 2, 3):
-        for h in range(2):
-            wire.arrived(("q", 1, dz, h))
+    for i in (0, 2):
+        for dz in (1, 3):
+            wire.arrived(("q", 1, dz, i))
+    for j in range(4):
+        wire.arrived(("q", 1, 2, j))
     for dz in range(4):
         spread_query(4 + dz)
 
@@ -434,7 +431,8 @@
         refs = refs[3:]
     if starts:
         sub_ref = refs.pop(0)
-        mask = refs.pop()
+        mask, x_own = refs[-2:]
+        refs = refs[:-2]
     send_sem, recv_sem, copy_sem = refs[:3]
     refs = refs[3:]
     place = Place()
@@ -458,9 +456,12 @@
         copies.append(copy)
         return copy
 
+    if starts:
+        x_ready = load(x_ref, x_own)
+        x_ref = x_own
     if reduces:
-        got, mix, spare, w_out, w_up, w_down = refs[:6]
-        refs = refs[6:]
+        got, mix, w_out, w_up, w_down = refs[:5]
+        refs = refs[5:]
         mix_ready = [
             load(w_out_h.at[layer], w_out),
             load(w_up_h.at[layer], w_up),
@@ -476,10 +477,12 @@
         pl.semaphore_signal(barrier, inc=1, device_id=peer, device_id_type=MESH)
     pl.semaphore_wait(barrier, len(peers))
     wire = Wire(send_sem, recv_sem)
+    if starts:
+        x_ready.wait()
     if reduces:
         x_out[...] = reduce_and_mix(
             wire, peers[:3], a_ref, got, mix, x_ref, (w_out, w_up, w_down, mix_ready),
-            gain_ref[layer], bias_ref[layer], spare,
+            gain_ref[layer], bias_ref[layer],
         )
         x_ref = x_out
     if gathers:
@@ -497,10 +500,10 @@
     reduces, gathers = reduce_args is not None, w_qkv is not None
     vmem = pl.BlockSpec(memory_space=pltpu.VMEM)
     hbm = pl.BlockSpec(memory_space=pltpu.HBM)
-    args, specs, outs = [x], [vmem], []
+    args, specs, outs = [x], [vmem if reduces else hbm], []
     scratch = [
-        pltpu.SemaphoreType.DMA((14 * reduces + 44 * gathers,)),
-        pltpu.SemaphoreType.DMA((14 * reduces + 44 * gathers,)),
+        pltpu.SemaphoreType.DMA((20 * reduces + 57 * gathers,)),
+        pltpu.SemaphoreType.DMA((20 * reduces + 57 * gathers,)),
         pltpu.SemaphoreType.DMA((4,)),
     ]
     bf16 = jnp.bfloat16
@@ -509,9 +512,8 @@
         specs += [vmem, hbm, hbm, hbm, vmem, vmem]
         outs.append(jax.ShapeDtypeStruct((128, 512), bf16))
         scratch += [
-            pltpu.VMEM((14, PACK, 128), bf16),
-            pltpu.VMEM((6, PACK, 128), bf16),
-            pltpu.VMEM((512, 128), jnp.float32),
+            pltpu.VMEM((28, PACK, 128), bf16),
+            pltpu.VMEM((12, PACK, 128), bf16),
             pltpu.VMEM((512, 512), bf16),
             pltpu.VMEM((512, 1024), bf16),
             pltpu.VMEM((1024, 512), bf16),
@@ -536,7 +538,7 @@
         specs.append(hbm)
         outs.append(jax.ShapeDtypeStruct((NQ, NK), jnp.int32))
         out_specs.append(pl.BlockSpec(memory_space=pltpu.SMEM))
-        scratch.append(pltpu.SMEM((128, 128), jnp.int32))
+        scratch += [pltpu.SMEM((128, 128), jnp.int32), pltpu.VMEM((128, 512), bf16)]
     return pl.pallas_call(
         functools.partial(link_kernel, layer, reduces, gathers),
         out_shape=tuple(outs),
@@ -551,7 +553,12 @@
 
 def per_device(node_feats, block_mask, w_qkv, w_out, w_up, w_down, ln_gain, ln_bias):
     x = node_feats
-    q, k, vt, sub = link(-1, x, w_qkv=w_qkv, block_mask=block_mask)
+    w_qkv, w_out, w_up, w_down, block_mask = (
+        pltpu.with_memory_space_constraint(a, pltpu.HBM)
+        for a in (w_qkv, w_out, w_up, w_down, block_mask)
+    )
+    x_first = pltpu.with_memory_space_constraint(x, pltpu.HBM)
+    q, k, vt, sub = link(-1, x_first, w_qkv=w_qkv, block_mask=block_mask)
     for layer in range(LAYERS):
         parts = attention(sub, q, k, vt)
         last = layer == LAYERS - 1

time: 82 us -> 76.5 us (0.933)
  local copies, waits for them, and re-layouts: 4.32 us -> 0.68 us
  Pallas kernels: 78.4 us -> 76.3 us
    pallas_call x3, Pallas kernels: 71.6 us -> 65.2 us  [link(): pl.pallas_call(functools.partial(link_kernel, layer, reduces, gathers), o...]
    pallas_call x2, Pallas kernels: 6.85 us -> 11.1 us  [attention(): pl.pallas_call(attention_kernel, out_shape=pltpu.VMEM((NQ, 4, PACK, 128),...]
    unnamed x17 -> x7, local copies, waits for them, and re-layouts: 4.32 us -> 0.68 us
where the time goes in v4:
time: 76.5 us; the launch traced here: 77.1 us
  Pallas kernels  76.3 us (100%)
    pallas_call x3, Pallas kernels, link(): pl.pallas_call(functools.partial(link_kernel, layer, reduces, gathers), o...  65.2 us
    pallas_call x2, Pallas kernels, attention(): pl.pallas_call(attention_kernel, out_shape=pltpu.VMEM((NQ, 4, PACK, 128),...  11.1 us

profile of v4, /device:TPU:0, one launch (start us, length us, event | category | flops | bytes accessed | tf_op | source)
XLA Modules:
  0.0 77.1 jit_solution(5967469267819344759)
XLA Ops:
  0.0 21.0 %shard_map.82 = (bf16[8,4,128,256]{3,2,1,0:T(8,128)(2,1)S(1)}, bf16[16,128,512]{2,1,0:T(8,128)(2,1)S(1)}, bf16[16,512,128]{2,1,0:T(8,128)(2,1)S(1)}, s32[8,16]{1,0:T(8,128)S(1)}) custom-call(bf16[128,512]{1,0:T(8,128)(2,1)} %refs_0_.3, bf16[2,512,1536]{2,1,0:T(8,128)(2,1)} %refs_7_.1, s32[128,128]{1,0:T(8,128)} %refs_2_.3), custom_call_target="tpu_custom_call" | custom-call | tf_op jit(solution)/shard_map/pallas_call | solution.py:542
  21.0 0.0 copy-start
  21.0 0.0 copy-start.1
  21.0 0.0 copy-start.2
  21.1 5.6 %shard_map.83.refs_1_ = bf16[8,4,144,128]{3,2,1,0:T(8,128)(2,1)S(1)} custom-call(s32[8,16]{1,0:T(8,128)S(1)} %get-tuple-element.13.sub_ref, bf16[8,4,128,256]{3,2,1,0:T(8,128)(2,1)S(1)} %get-tuple-element.14.qd, bf16[16,128,512]{2,1,0:T(8,128)(2,1)S(1)} %get-tuple-element.15.k_ref, bf16[16,512,128]{2,1,0:T(8,128)(2,1)S(1)} %get-tuple-element.16.vt_ref), custom_call_target="tpu_custom_call" | custom-call | tf_op jit(solution)/shard_map/pallas_call | solution.py:139
  26.6 0.0 copy-done
  26.6 0.0 copy-done.1
  26.6 0.0 copy-done.2
  26.6 29.6 %shard_map.84 = (bf16[128,512]{1,0:T(8,128)(2,1)S(1)}, bf16[8,4,128,256]{3,2,1,0:T(8,128)(2,1)S(1)}, bf16[16,128,512]{2,1,0:T(8,128)(2,1)S(1)}, bf16[16,512,128]{2,1,0:T(8,128)(2,1)S(1)}) custom-call(bf16[128,512]{1,0:T(8,128)(2,1)S(1)} %copy-done, bf16[8,4,144,128]{3,2,1,0:T(8,128)(2,1)S(1)} %shard_map.83.refs_1_, bf16[2,512,512]{2,1,0:T(8,128)(2,1)} %refs_2_.5, ...), custom_call_target="tpu_custom_call" | custom-call | tf_op jit(solution)/shard_map/pallas_call | solution.py:542
  56.3 5.5 %shard_map.85.refs_1_ = bf16[8,4,144,128]{3,2,1,0:T(8,128)(2,1)S(1)} custom-call(s32[8,16]{1,0:T(8,128)S(1)} %get-tuple-element.13.sub_ref, bf16[8,4,128,256]{3,2,1,0:T(8,128)(2,1)S(1)} %get-tuple-element.18.qd, bf16[16,128,512]{2,1,0:T(8,128)(2,1)S(1)} %get-tuple-element.19.k_ref, bf16[16,512,128]{2,1,0:T(8,128)(2,1)S(1)} %get-tuple-element.20.vt_ref), custom_call_target="tpu_custom_call" | custom-call | tf_op jit(solution)/shard_map/pallas_call | solution.py:139
  61.8 14.6 %shard_map.86 = bf16[128,512]{1,0:T(8,128)(2,1)S(1)} custom-call(bf16[128,512]{1,0:T(8,128)(2,1)S(1)} %get-tuple-element.17.refs_0_, bf16[8,4,144,128]{3,2,1,0:T(8,128)(2,1)S(1)} %shard_map.85.refs_1_, bf16[2,512,512]{2,1,0:T(8,128)(2,1)} %refs_2_.5, bf16[2,512,1024]{2,1,0:T(8,128)(2,1)} %refs_3_.3, bf16[2,1024,512]{2,1,0:T(8,128)(2,1)} %refs_4_.3, ...), custom_call_target="tpu_custom_call" | custom-call | tf_op jit(solution)/shard_map/pallas_call | solution.py:542
  76.4 0.7 copy.10
Async XLA Ops:
  21.0 5.6 %copy-start = (bf16[128,512]{1,0:T(8,128)(2,1)S(1)}, bf16[128,512]{1,0:T(8,128)(2,1)}, u32[]{:S(2)}) copy-start(bf16[128,512]{1,0:T(8,128)(2,1)} %refs_0_.3) | copy-start | bytes 393220
  21.0 5.6 %copy-start.1 = (f32[2,2,512]{2,1,0:T(2,128)S(1)}, f32[2,2,512]{2,1,0:T(2,128)}, u32[]{:S(2)}) copy-start(f32[2,2,512]{2,1,0:T(2,128)} %refs_5_.3) | copy-start | bytes 24580
  21.0 5.6 %copy-start.2 = (f32[2,2,512]{2,1,0:T(2,128)S(1)}, f32[2,2,512]{2,1,0:T(2,128)}, u32[]{:S(2)}) copy-start(f32[2,2,512]{2,1,0:T(2,128)} %refs_6_.3) | copy-start | bytes 24580

commit v5 on v4

--- a/solution.py
+++ b/solution.py
@@ -47,76 +47,7 @@
     return parts[0:2] + parts[2:4] + parts[4:6]
 
 
-def attention_kernel(sub_ref, qd, k_ref, vt_ref, a_ref, order, scores_a, scores_b, tops_a, tops_b, peaks, masses, acc):
-    bank = ((scores_a, tops_a), (scores_b, tops_b))
-    count = jnp.int32(0)
-    for r in range(NQ):
-        for k in range(NK):
-            order[count] = 32 * r + k
-            count = count + sub_ref[r, k]
-        order[count] = order[jnp.maximum(count - 1, 0)] + 16
-        count = count + count % 2
-    units = count // 2
-    last = jnp.maximum(count - 1, 0)
-    tail = order[last]
-    order[count] = tail - tail % 32 + tail % 16 + 16
-    order[count + 1] = order[count]
-    peaks[...] = jnp.full_like(peaks, LOW)
-    masses[...] = jnp.zeros_like(masses)
-    acc[...] = jnp.zeros_like(acc)
-
-    def decode(u):
-        first, second = order[2 * u], order[2 * u + 1]
-        dead = [jnp.where((code // 16) % 2 == 1, LOW, 0.0) for code in (first, second)]
-        return first // 32, first % 16, second % 16, dead
-
-    def score(u, slot):
-        r, k0, k1, dead = decode(u)
-        scores, tops = bank[slot]
-        for p in range(4):
-            lanes = slice(128 * p, 128 * p + 128)
-            keys = jnp.concatenate([k_ref[k0, :, lanes], k_ref[k1, :, lanes]], axis=0)
-            s = dot_nn(keys, qd[r, p])
-            scores[p] = s
-            top = jnp.maximum(
-                jnp.max(s[0:128], axis=0, keepdims=True) + dead[0],
-                jnp.max(s[128:256], axis=0, keepdims=True) + dead[1],
-            )
-            tops[p : p + 1, :] = top
-
-    def absorb(u, slot):
-        r, k0, k1, dead = decode(u)
-        scores, tops = bank[slot]
-        before = peaks[r]
-        top = jnp.maximum(before, tops[...])
-        fade = jnp.exp2(before - top)
-        peaks[r] = top
-        sums = []
-        for p in range(4):
-            lanes = slice(128 * p, 128 * p + 128)
-            here = top[p : p + 1]
-            w0 = jnp.exp2(scores[p, 0:128] - (here - dead[0]))
-            w1 = jnp.exp2(scores[p, 128:256] - (here - dead[1]))
-            sums.append(jnp.sum(w0, axis=0, keepdims=True) + jnp.sum(w1, axis=0, keepdims=True))
-            w = jnp.concatenate([w0.astype(jnp.bfloat16), w1.astype(jnp.bfloat16)], axis=0)
-            values = jnp.concatenate([vt_ref[k0, lanes, :], vt_ref[k1, lanes, :]], axis=1)
-            o = dot_nn(values, w)
-            lo, hi = slice(128 * p, 128 * p + 64), slice(128 * p + 64, 128 * p + 128)
-            acc[r, lo, :] = acc[r, lo, :] * fade[p : p + 1, :128] + o[0:64, 0:128]
-            acc[r, hi, :] = acc[r, hi, :] * fade[p : p + 1, 128:] + o[64:128, 128:256]
-        masses[r] = masses[r] * fade + jnp.concatenate(sums, axis=0)
-
-    score(0, 0)
-
-    def two_units(i, carry):
-        u = 2 * i
-        score(u + 1, 1)
-        absorb(u, 0)
-        score(jnp.minimum(u + 2, units), 0)
-        absorb(u + 1, 1)
-        return carry
-
-    lax.fori_loop(0, (units + 1) // 2, two_units, 0)
+def finish_parts(peaks, masses, acc, a_ref):
     for r in range(NQ):
         mass, peak = masses[r], peaks[r]
         some = mass > 0.0
@@ -134,25 +65,107 @@
             a_ref[r, p, 128:PACK, :] = split_lse(pair)
 
 
+def attention_kernel(
+    sub_any, qd, k_ref, vt_ref, peaks, masses, acc,
+    sub_ref, sub_sem, order, scores_a, scores_b, tops_a, tops_b,
+):
+    sub_copy = pltpu.make_async_copy(sub_any, sub_ref, sub_sem)
+    sub_copy.start()
+    peaks[...] = jnp.full_like(peaks, LOW)
+    masses[...] = jnp.zeros_like(masses)
+    acc[...] = jnp.zeros_like(acc)
+    sub_copy.wait()
+    bank = ((scores_a, tops_a), (scores_b, tops_b))
+    count = jnp.int32(0)
+    for r in range(NQ):
+        for k in range(NK):
+            order[count] = 32 * r + k
+            count = count + sub_ref[r, k]
+        order[count] = order[jnp.maximum(count - 1, 0)] + 16
+        count = count + count % 2
+    units = count // 2
+    last = jnp.maximum(count - 1, 0)
+    tail = order[last]
+    order[count] = tail - tail % 32 + tail % 16 + 16
+    order[count + 1] = order[count]
+
+    def decode(u):
+        first, second = order[2 * u], order[2 * u + 1]
+        dead = [jnp.where((code // 16) % 2 == 1, LOW, 0.0) for code in (first, second)]
+        return first // 32, first % 16, second % 16, dead
+
+    def score(u, slot, p):
+        r, k0, k1, dead = decode(u)
+        scores, tops = bank[slot]
+        lanes = slice(128 * p, 128 * p + 128)
+        keys = jnp.concatenate([k_ref[k0, :, lanes], k_ref[k1, :, lanes]], axis=0)
+        s = dot_nn(keys, qd[r, p])
+        scores[p] = s
+        top = jnp.maximum(
+            jnp.max(s[0:128], axis=0, keepdims=True) + dead[0],
+            jnp.max(s[128:256], axis=0, keepdims=True) + dead[1],
+        )
+        tops[p : p + 1, :] = top
+
+    def absorb(u, slot, p):
+        r, k0, k1, dead = decode(u)
+        scores, tops = bank[slot]
+        before = peaks[r, p : p + 1, :]
+        here = jnp.maximum(before, tops[p : p + 1, :])
+        fade = jnp.exp2(before - here)
+        peaks[r, p : p + 1, :] = here
+        lanes = slice(128 * p, 128 * p + 128)
+        w0 = jnp.exp2(scores[p, 0:128] - (here - dead[0]))
+        w1 = jnp.exp2(scores[p, 128:256] - (here - dead[1]))
+        mass = jnp.sum(w0, axis=0, keepdims=True) + jnp.sum(w1, axis=0, keepdims=True)
+        w = jnp.concatenate([w0.astype(jnp.bfloat16), w1.astype(jnp.bfloat16)], axis=0)
+        values = jnp.concatenate([vt_ref[k0, lanes, :], vt_ref[k1, lanes, :]], axis=1)
+        o = dot_nn(values, w)
+        lo, hi = slice(128 * p, 128 * p + 64), slice(128 * p + 64, 128 * p + 128)
+        acc[r, lo, :] = acc[r, lo, :] * fade[:, :128] + o[0:64, 0:128]
+        acc[r, hi, :] = acc[r, hi, :] * fade[:, 128:] + o[64:128, 128:256]
+        masses[r, p : p + 1, :] = masses[r, p : p + 1, :] * fade + mass
+
+    for p in range(4):
+        score(0, 0, p)
+
+    def two_units(i, carry):
+        u = 2 * i
+        for p in range(4):
+            score(u + 1, 1, p)
+            absorb(u, 0, p)
+        for p in range(4):
+            score(jnp.minimum(u + 2, units), 0, p)
+            absorb(u + 1, 1, p)
+        return carry
+
+    lax.fori_loop(0, (units + 1) // 2, two_units, 0)
+
+
 def attention(sub, q, k, vt):
     vmem = pl.BlockSpec(memory_space=pltpu.VMEM)
     return pl.pallas_call(
         attention_kernel,
-        out_shape=pltpu.VMEM((NQ, 4, PACK, 128), jnp.bfloat16),
-        in_specs=[pl.BlockSpec(memory_space=pltpu.SMEM), vmem, vmem, vmem],
-        out_specs=vmem,
+        out_shape=(
+            pltpu.VMEM((NQ, 4, 256), jnp.float32),
+            pltpu.VMEM((NQ, 4, 256), jnp.float32),
+            pltpu.VMEM((NQ, 512, 128), jnp.float32),
+        ),
+        in_specs=[pl.BlockSpec(memory_space=pl.ANY), vmem, vmem, vmem],
+        out_specs=(vmem, vmem, vmem),
         scratch_shapes=[
+            pltpu.SMEM((NQ, NK), jnp.int32),
+            pltpu.SemaphoreType.DMA,
             pltpu.SMEM((NQ * NK + 4,), jnp.int32),
             pltpu.VMEM((4, 256, 256), jnp.float32),
             pltpu.VMEM((4, 256, 256), jnp.float32),
             pltpu.VMEM((4, 256), jnp.float32),
             pltpu.VMEM((4, 256), jnp.float32),
-            pltpu.VMEM((NQ, 4, 256), jnp.float32),
-            pltpu.VMEM((NQ, 4, 256), jnp.float32),
-            pltpu.VMEM((NQ, 512, 128), jnp.float32),
         ],
         compiler_params=pltpu.CompilerParams(vmem_limit_bytes=16 * 2**20),
     )(sub, q, k, vt)
+
+
 class Place:
     def __init__(self):
         row, col = lax.axis_index("row"), lax.axis_index("col")
@@ -291,7 +304,9 @@
     return layer_norm(hidden.astype(jnp.float32) + down, gain[1:2], bias[1:2]).astype(jnp.bfloat16)
 
 
-def gather_and_project(wire, peers, x_ref, xg, qg, w, wvt, ready, q_ref, k_ref, vt_ref):
+def gather_and_project(
+    wire, peers, x_ref, xg, qg, w, wvt, ready, aside, q_ref, k_ref, vt_ref
+):
     zp, zm, xq, yp, ym, xk, sib = peers
 
     def part(ref, j, n=1):
@@ -332,6 +347,8 @@
         for p in range(4):
             q_ref[s, p, 0:64, 128:256] = off
             q_ref[s, p, 64:128, 0:128] = off
+    if aside is not None:
+        aside()
 
     def project(slots):
         rows = jnp.concatenate([x_ref[...] if s == 0 else xg[s] for s in slots], axis=0)
@@ -351,15 +368,16 @@
         wire.send(("k", 0, 2, i), key(0, 0, 3, i, 1), key(0, 0, 2, i, 1), yp)
         wire.arrived(("k", 0, 1, 2 + i))
         wire.send(("k", 0, 2, 2 + i), key(0, 0, 1, 2 + i, 1), key(0, 0, 2, 2 + i, 1), ym)
+    for i in (0, 2):
+        wire.arrived(("k", 1, 0, i))
+        wire.send(("k", 1, 3, i), key(0, 1, 0, i, 2), key(0, 1, 3, i, 2), yp)
+        wire.send(("k", 1, 1, i), key(0, 1, 0, i, 2), key(0, 1, 1, i, 2), ym)
     for i in range(2):
         wire.arrived(("q", 0, 3, i))
         wire.send(("q", 0, 2, i), query(0, 3, i, 1), query(0, 2, i, 1), zp)
         wire.arrived(("q", 0, 1, 2 + i))
         wire.send(("q", 0, 2, 2 + i), query(0, 1, 2 + i, 1), query(0, 2, 2 + i, 1), zm)
     for i in (0, 2):
-        wire.arrived(("k", 1, 0, i))
-        wire.send(("k", 1, 3, i), key(0, 1, 0, i, 2), key(0, 1, 3, i, 2), yp)
-        wire.send(("k", 1, 1, i), key(0, 1, 0, i, 2), key(0, 1, 1, i, 2), ym)
         wire.arrived(("q", 1, 0, i))
         wire.send(("q", 1, 3, i), query(1, 0, i, 2), query(1, 3, i, 2), zp)
         wire.send(("q", 1, 1, i), query(1, 0, i, 2), query(1, 1, i, 2), zm)
@@ -418,8 +436,9 @@
     x_ref = refs.pop(0)
     starts = not reduces
     if reduces:
-        a_ref, w_out_h, w_up_h, w_down_h, gain_ref, bias_ref = refs[:6]
-        refs = refs[6:]
+        sums = refs[:3]
+        w_out_h, w_up_h, w_down_h, gain_ref, bias_ref = refs[3:8]
+        refs = refs[8:]
     if gathers:
         w_h = refs.pop(0)
     if starts:
@@ -460,8 +479,8 @@
         x_ready = load(x_ref, x_own)
         x_ref = x_own
     if reduces:
-        got, mix, w_out, w_up, w_down = refs[:5]
-        refs = refs[5:]
+        a_ref, got, mix, w_out, w_up, w_down = refs[:6]
+        refs = refs[6:]
         mix_ready = [
             load(w_out_h.at[layer], w_out),
             load(w_up_h.at[layer], w_up),
@@ -475,6 +494,8 @@
     barrier = pltpu.get_barrier_semaphore()
     for peer in peers:
         pl.semaphore_signal(barrier, inc=1, device_id=peer, device_id_type=MESH)
+    if reduces:
+        finish_parts(*sums, a_ref)
     pl.semaphore_wait(barrier, len(peers))
     wire = Wire(send_sem, recv_sem)
     if starts:
@@ -485,14 +506,17 @@
             gain_ref[layer], bias_ref[layer],
         )
         x_ref = x_out
-    if gathers:
-        gather_and_project(wire, peers, x_ref, xg, qg, w, wvt, w_ready, q_ref, k_ref, vt_ref)
-    if starts:
+    def slice_mask():
         mask_ready.wait()
         queries, keys = query_blocks(place), key_blocks(place)
         for i in range(NQ):
             for j in range(NK):
                 sub_ref[i, j] = mask[queries[i], keys[j]]
+
+    if gathers:
+        gather_and_project(
+            wire, peers, x_ref, xg, qg, w, wvt, w_ready, slice_mask if starts else None, q_ref, k_ref, vt_ref
+        )
     wire.drain()
 
 
@@ -509,9 +533,10 @@
     bf16 = jnp.bfloat16
     if reduces:
         args += list(reduce_args)
-        specs += [vmem, hbm, hbm, hbm, vmem, vmem]
+        specs += [vmem, vmem, vmem, hbm, hbm, hbm, vmem, vmem]
         outs.append(jax.ShapeDtypeStruct((128, 512), bf16))
         scratch += [
+            pltpu.VMEM((NQ, 4, PACK, 128), bf16),
             pltpu.VMEM((28, PACK, 128), bf16),
             pltpu.VMEM((12, PACK, 128), bf16),
             pltpu.VMEM((512, 512), bf16),
@@ -562,7 +587,7 @@
     for layer in range(LAYERS):
         parts = attention(sub, q, k, vt)
         last = layer == LAYERS - 1
-        rest = (parts, w_out, w_up, w_down, ln_gain, ln_bias)
+        rest = (*parts, w_out, w_up, w_down, ln_gain, ln_bias)
         if last:
             (x,) = link(layer, x, reduce_args=rest)
         else:

time: 76.5 us -> 76.2 us (level); the launches traced: 77.1 us -> 75 us
  Pallas kernels: 76.3 us -> 74.2 us
    pallas_call x2, Pallas kernels: 11.1 us -> 6.56 us  [attention(): pl.pallas_call(attention_kernel, out_shape=(pltpu.VMEM((NQ, 4, 256), jnp....]
    pallas_call x3, Pallas kernels: 65.2 us -> 67.7 us  [link(): pl.pallas_call(functools.partial(link_kernel, layer, reduces, gathers), o...]
where the time goes in v5:
time: 76.2 us; the launch traced here: 75 us
  Pallas kernels  74.2 us (97%)
    pallas_call x3, Pallas kernels, link(): pl.pallas_call(functools.partial(link_kernel, layer, reduces, gathers), o...  67.7 us
    pallas_call x2, Pallas kernels, attention(): pl.pallas_call(attention_kernel, out_shape=(pltpu.VMEM((NQ, 4, 256), jnp....  6.56 us

profile of v5, /device:TPU:0, one launch (start us, length us, event | category | flops | bytes accessed | tf_op | source)
XLA Modules:
  0.0 75.0 jit_solution(173499136543611525)
XLA Ops:
  0.0 21.0 %shard_map.82 = (bf16[8,4,128,256]{3,2,1,0:T(8,128)(2,1)S(1)}, bf16[16,128,512]{2,1,0:T(8,128)(2,1)S(1)}, bf16[16,512,128]{2,1,0:T(8,128)(2,1)S(1)}, s32[8,16]{1,0:T(8,128)S(1)}) custom-call(bf16[128,512]{1,0:T(8,128)(2,1)} %refs_0_.3, bf16[2,512,1536]{2,1,0:T(8,128)(2,1)} %refs_9_.1, s32[128,128]{1,0:T(8,128)} %refs_2_.1), custom_call_target="tpu_custom_call" | custom-call | tf_op jit(solution)/shard_map/pallas_call | solution.py:567
  21.0 0.0 copy-start
  21.0 0.0 copy-start.1
  21.1 0.0 copy-start.2
  21.1 3.2 %shard_map.83 = (f32[8,4,256]{2,1,0:T(4,128)S(1)}, f32[8,4,256]{2,1,0:T(4,128)S(1)}, f32[8,512,128]{2,1,0:T(8,128)S(1)}) custom-call(s32[8,16]{1,0:T(8,128)S(1)} %get-tuple-element.19.sub_any, bf16[8,4,128,256]{3,2,1,0:T(8,128)(2,1)S(1)} %get-tuple-element.20.qd, bf16[16,128,512]{2,1,0:T(8,128)(2,1)S(1)} %get-tuple-element.21.k_ref, ...), custom_call_target="tpu_custom_call" | custom-call | tf_op jit(solution)/shard_map/pallas_call | solution.py:147
  24.3 0.0 copy-done
  24.3 0.0 copy-done.1
  24.3 0.0 copy-done.2
  24.3 30.3 %shard_map.84 = (bf16[128,512]{1,0:T(8,128)(2,1)S(1)}, bf16[8,4,128,256]{3,2,1,0:T(8,128)(2,1)S(1)}, bf16[16,128,512]{2,1,0:T(8,128)(2,1)S(1)}, bf16[16,512,128]{2,1,0:T(8,128)(2,1)S(1)}) custom-call(bf16[128,512]{1,0:T(8,128)(2,1)S(1)} %copy-done, f32[8,4,256]{2,1,0:T(4,128)S(1)} %get-tuple-element.23.refs_1_, f32[8,4,256]{2,1,0:T(4,128)S(1)} %get-tuple-element.24.refs_2_, ...), custom_call_target="tpu_custom_call" | custom-call | tf_op jit(solution)/shard_map/pallas_call | solution.py:567
  54.7 3.3 %shard_map.85 = (f32[8,4,256]{2,1,0:T(4,128)S(1)}, f32[8,4,256]{2,1,0:T(4,128)S(1)}, f32[8,512,128]{2,1,0:T(8,128)S(1)}) custom-call(s32[8,16]{1,0:T(8,128)S(1)} %get-tuple-element.19.sub_any, bf16[8,4,128,256]{3,2,1,0:T(8,128)(2,1)S(1)} %get-tuple-element.27.qd, bf16[16,128,512]{2,1,0:T(8,128)(2,1)S(1)} %get-tuple-element.28.k_ref, ...), custom_call_target="tpu_custom_call" | custom-call | tf_op jit(solution)/shard_map/pallas_call | solution.py:147
  58.0 16.3 %shard_map.86 = bf16[128,512]{1,0:T(8,128)(2,1)S(1)} custom-call(bf16[128,512]{1,0:T(8,128)(2,1)S(1)} %get-tuple-element.26.refs_0_, f32[8,4,256]{2,1,0:T(4,128)S(1)} %get-tuple-element.30.refs_1_, f32[8,4,256]{2,1,0:T(4,128)S(1)} %get-tuple-element.31.refs_2_, f32[8,512,128]{2,1,0:T(8,128)S(1)} %get-tuple-element.32.refs_3_, bf16[2,512,512]{2,1,0:T(8,128)(2,1)} %refs_4_.3, ...), custom_call_target="tpu_custom_call" | custom-call | tf_op jit(solution)/shard_map/pallas_call | solution.py:567
  74.3 0.7 copy.10
Async XLA Ops:
  21.0 3.3 %copy-start = (bf16[128,512]{1,0:T(8,128)(2,1)S(1)}, bf16[128,512]{1,0:T(8,128)(2,1)}, u32[]{:S(2)}) copy-start(bf16[128,512]{1,0:T(8,128)(2,1)} %refs_0_.3) | copy-start | bytes 393220
  21.0 3.3 %copy-start.1 = (f32[2,2,512]{2,1,0:T(2,128)S(1)}, f32[2,2,512]{2,1,0:T(2,128)}, u32[]{:S(2)}) copy-start(f32[2,2,512]{2,1,0:T(2,128)} %refs_7_.3) | copy-start | bytes 24580
  21.1 3.3 %copy-start.2 = (f32[2,2,512]{2,1,0:T(2,128)S(1)}, f32[2,2,512]{2,1,0:T(2,128)}, u32[]{:S(2)}) copy-start(f32[2,2,512]{2,1,0:T(2,128)} %refs_8_.3) | copy-start | bytes 24580

commit v6 on v5

--- a/solution.py
+++ b/solution.py
@@ -307,7 +307,7 @@
 def gather_and_project(
     wire, peers, x_ref, xg, qg, w, wvt, ready, aside, q_ref, k_ref, vt_ref
 ):
-    zp, zm, xq, yp, ym, xk, sib = peers
+    zp, zm, xq, yp, ym, xk, sib, yf, zf = peers
 
     def part(ref, j, n=1):
         return ref.at[pl.ds(32 * j, 32 * n)]
@@ -321,12 +321,26 @@
     def across(dx, dy, j=0, n=4):
         wire.send(("s", dx, dy, j), key(0, dx, dy, j, n), key(1, dx, dy, j, n), sib)
 
-    for i in range(4):
-        j = (i + 2) % 4
-        wire.send(("k", 0, 3, i), part(x_ref, i), key(0, 0, 3, i, 1), yp)
-        wire.send(("k", 0, 1, j), part(x_ref, j), key(0, 0, 1, j, 1), ym)
-        if i % 2 == 0:
-            wire.send(("k", 1, 0, i), part(x_ref, i, 2), key(0, 1, 0, i, 2), xk)
+    def start(name, source, at, far, plus, minus, pair):
+        for d, h, to in ((2, 0, far), (0, 2, pair), (3, 0, plus), (1, 0, minus),
+                         (0, 0, pair), (2, 2, far), (3, 2, plus), (1, 2, minus)):
+            dx = 1 if d == 0 else 0
+            wire.send((name, dx, d, h), source(h), at(dx, d, h, 2), to)
+
+    def relay(name, at, far, plus, minus, pair):
+        wire.arrived((name, 1, 0, 2))
+        for d, to in ((2, far), (3, plus), (1, minus)):
+            wire.send((name, 1, d, 2), at(1, 0, 2, 2), at(1, d, 2, 2), to)
+
+    def relay_pair(name, at, pair):
+        for d in (2, 3, 1):
+            wire.arrived((name, 0, d, 0))
+            wire.send((name, 1, d, 0), at(0, d, 0, 2), at(1, d, 0, 2), pair)
+
+    def key0(dx, dy, j, n):
+        return key(0, dx, dy, j, n)
+
+    start("k", lambda h: part(x_ref, h, 2), key0, yf, yp, ym, xk)
     wire.send(("s", 0, 0, 0), part(x_ref, 0, 4), key(1, 0, 0), sib)
     for i in ready:
         i.wait()
@@ -335,12 +349,7 @@
         qg[0, 128 * i : 128 * i + 128, :] = jnp.transpose(q[:, 128 * i : 128 * i + 128]).astype(
             jnp.bfloat16
         )
-    for i in range(4):
-        j = (i + 2) % 4
-        wire.send(("q", 0, 3, i), query(0, 0, i, 1), query(0, 3, i, 1), zp)
-        wire.send(("q", 0, 1, j), query(0, 0, j, 1), query(0, 1, j, 1), zm)
-        if i % 2 == 0:
-            wire.send(("q", 1, 0, i), query(0, 0, i, 2), query(1, 0, i, 2), xq)
+    start("q", lambda h: query(0, 0, h, 2), query, zf, zp, zm, xq)
     wvt[...] = jnp.transpose(w[:, 1024:1536].astype(jnp.float32)).astype(jnp.bfloat16)
     off = jnp.zeros((64, 128), jnp.bfloat16)
     for s in range(NQ):
@@ -363,70 +372,43 @@
             q_ref[s, p, 0:64, 0:128] = qg[s, 128 * p : 128 * p + 64, :]
             q_ref[s, p, 64:128, 128:256] = qg[s, 128 * p + 64 : 128 * p + 128, :]
 
-    for i in range(2):
-        wire.arrived(("k", 0, 3, i))
-        wire.send(("k", 0, 2, i), key(0, 0, 3, i, 1), key(0, 0, 2, i, 1), yp)
-        wire.arrived(("k", 0, 1, 2 + i))
-        wire.send(("k", 0, 2, 2 + i), key(0, 0, 1, 2 + i, 1), key(0, 0, 2, 2 + i, 1), ym)
-    for i in (0, 2):
-        wire.arrived(("k", 1, 0, i))
-        wire.send(("k", 1, 3, i), key(0, 1, 0, i, 2), key(0, 1, 3, i, 2), yp)
-        wire.send(("k", 1, 1, i), key(0, 1, 0, i, 2), key(0, 1, 1, i, 2), ym)
-    for i in range(2):
-        wire.arrived(("q", 0, 3, i))
-        wire.send(("q", 0, 2, i), query(0, 3, i, 1), query(0, 2, i, 1), zp)
-        wire.arrived(("q", 0, 1, 2 + i))
-        wire.send(("q", 0, 2, 2 + i), query(0, 1, 2 + i, 1), query(0, 2, 2 + i, 1), zm)
-    for i in (0, 2):
-        wire.arrived(("q", 1, 0, i))
-        wire.send(("q", 1, 3, i), query(1, 0, i, 2), query(1, 3, i, 2), zp)
-        wire.send(("q", 1, 1, i), query(1, 0, i, 2), query(1, 1, i, 2), zm)
+    relay("k", key0, yf, yp, ym, xk)
+    relay("q", query, zf, zp, zm, xq)
+    relay_pair("k", key0, xk)
+    relay_pair("q", query, xq)
+    wire.arrived(("k", 1, 0, 0))
     across(1, 0)
-    for i in range(2):
-        wire.arrived(("k", 0, 3, 2 + i))
-        wire.arrived(("k", 0, 1, i))
-    across(0, 3)
-    across(0, 1)
+    for d in (2, 3, 1):
+        wire.arrived(("k", 0, d, 2))
+        across(0, d)
     wire.arrived(("s", 0, 0, 0))
     project((0, 8))
-    for j in (0, 2, 1, 3):
-        wire.arrived(("k", 0, 2, j))
-        wire.send(("k", 1, 2, j), key(0, 0, 2, j, 1), key(0, 1, 2, j, 1), xk)
-    across(0, 2)
-    for j in (0, 2, 1, 3):
-        wire.arrived(("q", 0, 2, j))
-        wire.send(("q", 1, 2, j), query(0, 2, j, 1), query(1, 2, j, 1), xq)
     project((1, 3))
     project((2, 4))
-    for i in range(2):
-        wire.arrived(("q", 0, 3, 2 + i))
-        wire.arrived(("q", 0, 1, i))
+    for h in (2, 0):
+        for d in (2, 3, 1):
+            wire.arrived(("k", 1, d, h))
+            across(1, d, h, 2)
+    wire.arrived(("q", 1, 0, 0))
+    for d in (2, 3, 1):
+        wire.arrived(("q", 0, d, 2))
     for dz in range(4):
         spread_query(dz)
     for dx, dy in ((1, 0), (0, 3), (0, 1), (0, 2)):
         wire.arrived(("s", dx, dy, 0))
     project((9, 11))
-    for i in (0, 2):
-        for dy in (1, 3):
-            wire.arrived(("k", 1, dy, i))
-            across(1, dy, i, 2)
     project((10, 12))
-    for j in (0, 2, 1, 3):
-        wire.arrived(("k", 1, 2, j))
-        across(1, 2, j, 1)
     project((5, 7))
-    for i in (0, 2):
-        for dy in (1, 3):
-            wire.arrived(("s", 1, dy, i))
+    for h in (2, 0):
+        for d in (1, 3):
+            wire.arrived(("s", 1, d, h))
     project((13, 15))
-    for j in (0, 2, 1, 3):
-        wire.arrived(("s", 1, 2, j))
+    for h in (2, 0):
+        wire.arrived(("s", 1, 2, h))
     project((6, 14))
-    for i in (0, 2):
-        for dz in (1, 3):
-            wire.arrived(("q", 1, dz, i))
-    for j in range(4):
-        wire.arrived(("q", 1, 2, j))
+    for h in (2, 0):
+        for d in (2, 3, 1):
+            wire.arrived(("q", 1, d, h))
     for dz in range(4):
         spread_query(4 + dz)
 
@@ -466,6 +448,8 @@
             place.at(y=place.y + 3),
             place.at(x=place.x + 1 - 2 * (place.x % 2)),
             place.at(core=1 - place.core),
+            place.at(y=place.y + 2),
+            place.at(z=place.z + 2),
         ]
     copies = []
 
@@ -526,8 +510,8 @@
     hbm = pl.BlockSpec(memory_space=pltpu.HBM)
     args, specs, outs = [x], [vmem if reduces else hbm], []
     scratch = [
-        pltpu.SemaphoreType.DMA((20 * reduces + 57 * gathers,)),
-        pltpu.SemaphoreType.DMA((20 * reduces + 57 * gathers,)),
+        pltpu.SemaphoreType.DMA((20 * reduces + 41 * gathers,)),
+        pltpu.SemaphoreType.DMA((20 * reduces + 41 * gathers,)),
         pltpu.SemaphoreType.DMA((4,)),
     ]
     bf16 = jnp.bfloat16

time: 76.2 us -> 74.5 us (0.978); the launches traced: 75 us -> 75.2 us
    pallas_call x3, Pallas kernels: 67.7 us -> 69.4 us  [link(): pl.pallas_call(functools.partial(link_kernel, layer, reduces, gathers), o...]
    pallas_call x2, Pallas kernels: 6.56 us -> 5.01 us  [attention(): pl.pallas_call(attention_kernel, out_shape=(pltpu.VMEM((NQ, 4, 256), jnp....]
where the time goes in v6:
time: 74.5 us; the launch traced here: 75.2 us
  Pallas kernels  74.4 us (100%)
    pallas_call x3, Pallas kernels, link(): pl.pallas_call(functools.partial(link_kernel, layer, reduces, gathers), o...  69.4 us
    pallas_call x2, Pallas kernels, attention(): pl.pallas_call(attention_kernel, out_shape=(pltpu.VMEM((NQ, 4, 256), jnp....  5.01 us

profile of v6, /device:TPU:0, one launch (start us, length us, event | category | flops | bytes accessed | tf_op | source)
XLA Modules:
  0.0 75.2 jit_solution(6831066657569158602)
XLA Ops:
  0.0 20.0 %shard_map.82 = (bf16[8,4,128,256]{3,2,1,0:T(8,128)(2,1)S(1)}, bf16[16,128,512]{2,1,0:T(8,128)(2,1)S(1)}, bf16[16,512,128]{2,1,0:T(8,128)(2,1)S(1)}, s32[8,16]{1,0:T(8,128)S(1)}) custom-call(bf16[128,512]{1,0:T(8,128)(2,1)} %refs_0_.3, bf16[2,512,1536]{2,1,0:T(8,128)(2,1)} %refs_9_.1, s32[128,128]{1,0:T(8,128)} %refs_2_.1), custom_call_target="tpu_custom_call" | custom-call | tf_op jit(solution)/shard_map/pallas_call | solution.py:551
  20.1 0.0 copy-start
  20.1 0.0 copy-start.1
  20.1 0.0 copy-start.2
  20.1 2.5 %shard_map.83 = (f32[8,4,256]{2,1,0:T(4,128)S(1)}, f32[8,4,256]{2,1,0:T(4,128)S(1)}, f32[8,512,128]{2,1,0:T(8,128)S(1)}) custom-call(s32[8,16]{1,0:T(8,128)S(1)} %get-tuple-element.19.sub_any, bf16[8,4,128,256]{3,2,1,0:T(8,128)(2,1)S(1)} %get-tuple-element.20.qd, bf16[16,128,512]{2,1,0:T(8,128)(2,1)S(1)} %get-tuple-element.21.k_ref, ...), custom_call_target="tpu_custom_call" | custom-call | tf_op jit(solution)/shard_map/pallas_call | solution.py:147
  22.6 0.0 copy-done
  22.6 0.0 copy-done.1
  22.6 0.0 copy-done.2
  22.7 31.5 %shard_map.84 = (bf16[128,512]{1,0:T(8,128)(2,1)S(1)}, bf16[8,4,128,256]{3,2,1,0:T(8,128)(2,1)S(1)}, bf16[16,128,512]{2,1,0:T(8,128)(2,1)S(1)}, bf16[16,512,128]{2,1,0:T(8,128)(2,1)S(1)}) custom-call(bf16[128,512]{1,0:T(8,128)(2,1)S(1)} %copy-done, f32[8,4,256]{2,1,0:T(4,128)S(1)} %get-tuple-element.23.refs_1_, f32[8,4,256]{2,1,0:T(4,128)S(1)} %get-tuple-element.24.refs_2_, ...), custom_call_target="tpu_custom_call" | custom-call | tf_op jit(solution)/shard_map/pallas_call | solution.py:551
  54.1 2.5 %shard_map.85 = (f32[8,4,256]{2,1,0:T(4,128)S(1)}, f32[8,4,256]{2,1,0:T(4,128)S(1)}, f32[8,512,128]{2,1,0:T(8,128)S(1)}) custom-call(s32[8,16]{1,0:T(8,128)S(1)} %get-tuple-element.19.sub_any, bf16[8,4,128,256]{3,2,1,0:T(8,128)(2,1)S(1)} %get-tuple-element.27.qd, bf16[16,128,512]{2,1,0:T(8,128)(2,1)S(1)} %get-tuple-element.28.k_ref, ...), custom_call_target="tpu_custom_call" | custom-call | tf_op jit(solution)/shard_map/pallas_call | solution.py:147
  56.6 17.9 %shard_map.86 = bf16[128,512]{1,0:T(8,128)(2,1)S(1)} custom-call(bf16[128,512]{1,0:T(8,128)(2,1)S(1)} %get-tuple-element.26.refs_0_, f32[8,4,256]{2,1,0:T(4,128)S(1)} %get-tuple-element.30.refs_1_, f32[8,4,256]{2,1,0:T(4,128)S(1)} %get-tuple-element.31.refs_2_, f32[8,512,128]{2,1,0:T(8,128)S(1)} %get-tuple-element.32.refs_3_, bf16[2,512,512]{2,1,0:T(8,128)(2,1)} %refs_4_.3, ...), custom_call_target="tpu_custom_call" | custom-call | tf_op jit(solution)/shard_map/pallas_call | solution.py:551
  74.5 0.7 copy.10
Async XLA Ops:
  20.1 2.6 %copy-start = (bf16[128,512]{1,0:T(8,128)(2,1)S(1)}, bf16[128,512]{1,0:T(8,128)(2,1)}, u32[]{:S(2)}) copy-start(bf16[128,512]{1,0:T(8,128)(2,1)} %refs_0_.3) | copy-start | bytes 393220
  20.1 2.6 %copy-start.1 = (f32[2,2,512]{2,1,0:T(2,128)S(1)}, f32[2,2,512]{2,1,0:T(2,128)}, u32[]{:S(2)}) copy-start(f32[2,2,512]{2,1,0:T(2,128)} %refs_7_.3) | copy-start | bytes 24580
  20.1 2.6 %copy-start.2 = (f32[2,2,512]{2,1,0:T(2,128)S(1)}, f32[2,2,512]{2,1,0:T(2,128)}, u32[]{:S(2)}) copy-start(f32[2,2,512]{2,1,0:T(2,128)} %refs_8_.3) | copy-start | bytes 24580
